TPU v7x, 32 devices: a 4x4x1 block of a 4x4x8 slice. The times are simulated.
32 devices in a mesh: rep: 1 (over z), dp: 4 (over y), ad: 8 (over x, core).
Axes of the slice: x: 4, y: 4, z: 1, core: 2. Of those that a mesh axis runs over, the one named last changes fastest.
The devices are a block of a 4x4x8 slice.
Arguments:
- x_rows: bfloat16 [16384, 1536], P(('rep', 'dp', 'ad'))
- adapter_id: int32 [16384], P(('rep', 'dp', 'ad'))
- w_gate: bfloat16 [1536, 8960], replicated
- w_up: bfloat16 [1536, 8960], replicated
- w_down: bfloat16 [8960, 1536], replicated
- a_gate: bfloat16 [32, 1536, 128], P('ad')
- b_gate: bfloat16 [32, 128, 8960], P('ad')
- a_up: bfloat16 [32, 1536, 128], P('ad')
- b_up: bfloat16 [32, 128, 8960], P('ad')
- a_down: bfloat16 [32, 8960, 128], P('ad')
- b_down: bfloat16 [32, 128, 1536], P('ad')
Outputs:
- output: bfloat16 [16384, 1536], P(('rep', 'dp', 'ad'))
All inputs are finite; a program needn't handle non-finite values.
Results may differ from a plain program's by a relative error of at most 0.00166.
Values are sent between devices in bfloat16 or wider.
A program may use at most 768 MiB of HBM per device.

v0:
```python
import jax
import jax.numpy as jnp
from jax import lax
from jax.sharding import PartitionSpec as P

value_a10 = 32
CAP_MULT = 4


def route_plan(adapter_id, n_rows, group, n_local, capacity):
    owner = adapter_id // n_local
    tok_order = jnp.argsort(owner, stable=True)
    owner_sorted = jnp.take(owner, tok_order)
    counts = jnp.bincount(owner, length=group)
    starts = jnp.cumsum(counts) - counts
    slot_sorted = owner_sorted * capacity + jnp.arange(n_rows) - jnp.take(starts, owner_sorted)
    token_slot = jnp.take(slot_sorted, jnp.argsort(tok_order))
    within = jnp.arange(capacity)
    pick_index = jnp.minimum(starts[:, None] + within[None, :], n_rows - 1).reshape(-1)
    send_rows = jnp.take(tok_order, pick_index)
    filled = (within[None, :] < counts[:, None]).reshape(-1)
    send_local = jnp.where(filled, jnp.take(adapter_id, send_rows) % n_local, 0)
    return token_slot, send_rows, send_local


def solution(mesh):
    group = mesh.shape["ad"]
    tok_axes = ("rep", "dp", "ad")
    row_spec = P(tok_axes, None)
    owned = P("ad", None, None)

    def local_step(x_rows, adapter_id, w_gate, w_up, w_down, a_gate, b_gate, a_up, b_up, a_down, b_down):
        n_rows = x_rows.shape[0]
        n_local, _, rank = a_gate.shape
        d_ff = w_gate.shape[1]
        scale = value_a10 / rank
        capacity = (n_rows // group) * min(CAP_MULT, max(1, group // 2))
        token_slot, send_rows, send_local = route_plan(adapter_id, n_rows, group, n_local, capacity)
        local_recv = lax.all_to_all(send_local, "ad", 0, 0, tiled=True)
        select = (local_recv[:, None] == jnp.arange(n_local)[None, :]).astype(jnp.bfloat16)

        def low_rank(rows_in, a_mat, b_mat):
            low_proj = jnp.einsum("mk,akr->mar", rows_in, a_mat, preferred_element_type=jnp.float32)
            low_proj = low_proj.astype(jnp.bfloat16) * select[:, :, None]
            wide_proj = jnp.einsum("mar,arn->mn", low_proj, b_mat, preferred_element_type=jnp.float32)
            return (scale * wide_proj).astype(jnp.bfloat16)

        x_recv = lax.all_to_all(jnp.take(x_rows, send_rows, axis=0), "ad", 0, 0, tiled=True)
        gu_delta = jnp.concatenate([low_rank(x_recv, a_gate, b_gate), low_rank(x_recv, a_up, b_up)], axis=1)
        gu_token = jnp.take(lax.all_to_all(gu_delta, "ad", 0, 0, tiled=True), token_slot, axis=0)
        gate_pre = jnp.dot(x_rows, w_gate, preferred_element_type=jnp.float32) + gu_token[:, :d_ff].astype(jnp.float32)
        up_proj = jnp.dot(x_rows, w_up, preferred_element_type=jnp.float32) + gu_token[:, d_ff:].astype(jnp.float32)
        hidden = (jax.nn.silu(gate_pre) * up_proj).astype(jnp.bfloat16)
        h_recv = lax.all_to_all(jnp.take(hidden, send_rows, axis=0), "ad", 0, 0, tiled=True)
        down_delta = lax.all_to_all(low_rank(h_recv, a_down, b_down), "ad", 0, 0, tiled=True)
        down_token = jnp.take(down_delta, token_slot, axis=0)
        down_proj = jnp.dot(hidden, w_down, preferred_element_type=jnp.float32) + down_token.astype(jnp.float32)
        return (x_rows.astype(jnp.float32) + down_proj).astype(jnp.bfloat16)

    return jax.shard_map(local_step, mesh=mesh,
                         in_specs=(row_spec, P(tok_axes), P(), P(), P(), owned, owned, owned, owned, owned, owned),
                         out_specs=row_spec, check_vma=False)
```

profile of v0, /device:TPU:98, one launch (start us, length us, event | category | flops | bytes accessed | tf_op | source)
XLA Modules:
  0.0 1783.2 jit_solution(10302264397932480638)
XLA Ops:
  0.0 0.8 broadcast_maximum_fusion
  0.9 4.1 scatter_custom_fusion
  5.7 3.8 sort.34
  9.5 13.2 gather_fusion.6
  22.8 13.2 gather_fusion.7
  36.6 5.0 all-to-all-start.1
  41.6 10.1 gather_fusion
  51.8 6.1 broadcast_select_fusion.2
  57.9 5.5 all-to-all-start
  63.4 70.5 %all-to-all-done = bf16[8,256,1536]{2,1,0:T(8,128)(2,1)} async-done(((bf16[8,256,1536]{2,1,0:T(8,128)(2,1)}), bf16[8,256,1536]{2,1,0:T(8,128)(2,1)}, u32[]{:S(2)}, u32[]{:S(2)}) %all-to-all-start) | async-done | bytes 6291488 | tf_op jit(solution)/shard_map/all_to_all | solution.py:48
  133.9 7.1 fusion.6.clone.4
  141.0 5.5 fusion.5.clone.2
  146.5 27.1 %fusion = bf16[2048,8960]{1,0:T(8,128)(2,1)} fusion(bf16[4,128,8960]{2,1,0:T(8,128)(2,1)} %param.23, bf16[2048,4,128]{2,0,1:T(8,128)(2,1)} %fusion.6.clone.4), kind=kOutput, calls=%fused_computation.11 | convolution fusion | flops 18827182080 | bytes 47972352 | tf_op jit(solution)/shard_map/mar,arn->mn/dot_general | solution.py:45
  173.7 27.5 %fusion.1 = bf16[2048,8960]{1,0:T(8,128)(2,1)} fusion(bf16[4,128,8960]{2,1,0:T(8,128)(2,1)} %param.21, bf16[2048,4,128]{2,0,1:T(8,128)(2,1)S(1)} %fusion.5.clone.2), kind=kOutput, calls=%fused_computation.13 | convolution fusion | flops 18827182080 | bytes 47972352 | tf_op jit(solution)/shard_map/mar,arn->mn/dot_general | solution.py:45
  201.2 48.5 %pad_maximum_fusion = bf16[2048,17920]{1,0:T(8,128)(2,1)} fusion(bf16[2048,8960]{1,0:T(8,128)(2,1)} %fusion, bf16[2048,8960]{1,0:T(8,128)(2,1)} %fusion.1), kind=kLoop, calls=%fused_computation.9 | loop fusion | flops 146800640 | bytes 146800640 | tf_op jit(solution)/shard_map/concatenate | solution.py:49
  249.8 12.4 all-to-all-start.2
  262.2 3.5 gather_fusion.4
  265.7 3.8 sort.35
  270.1 4.9 fusion.15
  275.0 3.5 gather_fusion.5
  278.6 23.4 %fusion.21 = f32[512,8960]{1,0:T(8,128)} fusion(bf16[512,1536]{1,0:T(8,128)(2,1)S(1)} %copy-done.7, bf16[1536,8960]{1,0:T(8,128)(2,1)} %param.17), kind=kOutput, calls=%fused_computation.69 | convolution fusion | flops 14092861440 | bytes 47448064 | tf_op jit(solution)/shard_map/dot_general | solution.py:51
  302.0 749.9 %all-to-all-done.2 = bf16[8,256,17920]{2,1,0:T(8,128)(2,1)} async-done(((bf16[8,256,17920]{2,1,0:T(8,128)(2,1)}), bf16[8,256,17920]{2,1,0:T(8,128)(2,1)}, u32[]{:S(2)}, u32[]{:S(2)}) %all-to-all-start.2) | async-done | bytes 73400352 | tf_op jit(solution)/shard_map/all_to_all | solution.py:50
  1051.9 43.2 %gather_fusion.1 = bf16[512,17920]{1,0:T(8,128)(2,1)} fusion(bf16[2048,17920]{1,0:T(8,128)(2,1)} %bitcast.19, s32[1024]{0:T(1024)S(1)} %pad_clamp_fusion), kind=kCustom, calls=%fused_computation.5 | custom fusion | bytes 36702208 | tf_op jit(solution)/shard_map/jit(_take)/gather | solution.py:50
  1095.0 16.3 broadcast_select_fusion.1
  1111.3 34.1 %multiply_convert_fusion = bf16[512,8960]{1,0:T(8,128)(2,1)} fusion(f32[512,8960]{1,0:T(8,128)} %fusion.21, bf16[512,1536]{1,0:T(8,128)(2,1)S(1)} %copy-done.7, bf16[1536,8960]{1,0:T(8,128)(2,1)} %param.18, bf16[512,17920]{1,0:T(8,128)(2,1)} %broadcast_select_fusion.1), kind=kOutput, calls=%fused_computation.15 | convolution fusion | flops 14138736640 | bytes 74973184 | tf_op jit(solution)/shard_map/dot_general | solution.py:52
  1145.4 63.8 %gather_fusion.2 = bf16[2048,8960]{1,0:T(8,128)(2,1)} fusion(bf16[512,8960]{1,0:T(8,128)(2,1)} %multiply_convert_fusion, s32[2048]{0:T(1024)S(1)} %copy-done.10), kind=kCustom, calls=%fused_computation.6 | custom fusion | bytes 73408512 | tf_op jit(solution)/shard_map/jit(_take)/gather | solution.py:54
  1209.2 24.5 %broadcast_select_fusion = bf16[8,256,8960]{2,1,0:T(8,128)(2,1)} fusion(bf16[8,256,8960]{2,1,0:T(8,128)(2,1)} %bitcast.76, pred[8,256]{1,0:T(8,128)(4,1)S(1)} %copy-done.14), kind=kLoop, calls=%fused_computation.14 | loop fusion | flops 18350080 | bytes 73402368 | tf_op jit(solution)/shard_map/jit(_take)/select_n | solution.py:54
  1233.7 410.1 %all_to_all.51 = bf16[8,256,8960]{2,1,0:T(8,128)(2,1)} all-to-all(bf16[8,256,8960]{2,1,0:T(8,128)(2,1)} %broadcast_select_fusion), channel_id=1, replica_groups=mesh['rep'=1,'dp'=4,'ad'=8] {'ad'}, dimensions={0} | all-to-all | bytes 73400320 | tf_op jit(solution)/shard_map/all_to_all | solution.py:54
  1643.8 31.3 %fusion.2 = bf16[2048,1536]{1,0:T(8,128)(2,1)} fusion(bf16[4,128,1536]{2,1,0:T(8,128)(2,1)S(1)} %copy-done, bf16[2048,8960,1]{1,0,2:T(8,128)(2,1)} %bitcast.78, bf16[4,8960,128]{2,1,0:T(8,128)(2,1)} %param.24, bf16[2048,4]{0,1:T(4,128)(2,1)S(1)} %copy-done.16), kind=kOutput, calls=%fused_computation.18 | convolution fusion | flops 22020096000 | bytes 53755904 | tf_op jit(solution)/shard_map/mar,arn->mn/dot_general | solution.py:45
  1675.2 77.5 %all_to_all.52 = bf16[8,256,1536]{2,1,0:T(8,128)(2,1)} all-to-all(bf16[8,256,1536]{2,1,0:T(8,128)(2,1)} %bitcast.80), channel_id=1, replica_groups=mesh['rep'=1,'dp'=4,'ad'=8] {'ad'}, dimensions={0} | all-to-all | bytes 12582912 | tf_op jit(solution)/shard_map/all_to_all | solution.py:55
  1752.6 8.1 gather_fusion.3
  1760.8 22.0 %fusion.4 = bf16[512,1536]{1,0:T(8,128)(2,1)} fusion(bf16[512,8960]{1,0:T(8,128)(2,1)} %multiply_convert_fusion, bf16[8960,1536]{1,0:T(8,128)(2,1)} %param.19, bf16[512,1536]{1,0:T(8,128)(2,1)S(1)} %copy-done.8, bf16[512,1536]{1,0:T(8,128)(2,1)} %gather_fusion.3, pred[512]{0:T(512)(128)(4,1)S(1)} %copy-done.20), kind=kOutput, calls=%fused_computation.22 | convolution fusion | flops 14097580032 | bytes 41419264 | tf_op jit(solution)/shard_map/dot_general | solution.py:57
  (66 shorter events, 2.2 us)
Async XLA Ops:
  0.0 1643.8 %copy-start = (bf16[4,128,1536]{2,1,0:T(8,128)(2,1)S(1)}, bf16[4,128,1536]{2,1,0:T(8,128)(2,1)}, u32[]{:S(2)}) copy-start(bf16[4,128,1536]{2,1,0:T(8,128)(2,1)} %param.25) | copy-start | bytes 4718596
  0.0 22.7 %copy-start.3 = (s32[512]{0:T(512)S(1)}, s32[512]{0:T(512)}, u32[]{:S(2)}) copy-start(s32[512]{0:T(512)} %param.16) | copy-start | bytes 6148
  0.0 41.6 %copy-start.6 = (bf16[512,1536]{1,0:T(8,128)(2,1)S(1)}, bf16[512,1536]{1,0:T(8,128)(2,1)}, u32[]{:S(2)}) copy-start(bf16[512,1536]{1,0:T(8,128)(2,1)} %param.15) | copy-start | bytes 4718596
  0.9 50.9 %copy-start.4 = (s32[512]{0:T(512)}, s32[512]{0:T(512)S(1)}, u32[]{:S(2)}) copy-start(s32[512]{0:T(512)S(1)} %get-tuple-element.16) | copy-start | bytes 6148
  5.2 0.5 copy-start.11
  9.5 42.3 %copy-start.1 = (s32[512]{0:T(512)}, s32[512]{0:T(512)S(1)}, u32[]{:S(2)}) copy-start(s32[512]{0:T(512)S(1)} %get-tuple-element.9) | copy-start | bytes 6148
  22.8 29.0 %copy-start.9 = (s32[2048]{0:T(1024)}, s32[2048]{0:T(1024)S(1)}, u32[]{:S(2)}) copy-start(s32[2048]{0:T(1024)S(1)} %broadcast_clamp_fusion) | copy-start | bytes 24580
  36.6 21.3 %all-to-all-start.1 = ((s32[8,256,1]{1,2,0:T(1,128)}), s32[8,256,1]{1,2,0:T(1,128)S(1)}, u32[]{:S(2)}, u32[]{:S(2)}) async-start(s32[8,256,1]{1,2,0:T(1,128)} %bitcast.13), calls=%async_computation.1 | async-start | bytes 16384 | tf_op jit(solution)/shard_map/all_to_all | solution.py:39
  41.6 10.2 copy-start.13
  57.9 76.0 %all-to-all-start = ((bf16[8,256,1536]{2,1,0:T(8,128)(2,1)}), bf16[8,256,1536]{2,1,0:T(8,128)(2,1)}, u32[]{:S(2)}, u32[]{:S(2)}) async-start(bf16[8,256,1536]{2,1,0:T(8,128)(2,1)} %broadcast_select_fusion.2), calls=%async_computation | async-start | bytes 12582912 | tf_op jit(solution)/shard_map/all_to_all | solution.py:48
  63.4 77.6 %copy-start.15 = (bf16[2048,4]{0,1:T(4,128)(2,1)}, bf16[2048,4]{0,1:T(4,128)(2,1)S(1)}, u32[]{:S(2)}) copy-start(bf16[2048,4]{0,1:T(4,128)(2,1)S(1)} %fusion.10) | copy-start | bytes 49156
  133.9 7.1 copy-start.21
  249.8 12.4 copy-start.2
  249.8 12.4 copy-start.5
  249.8 19.7 %copy-start.12 = (s32[8]{0:T(128)S(1)}, s32[8]{0:T(128)}, u32[]{:S(2)}) copy-start(s32[8]{0:T(128)} %copy-done.11) | copy-start | bytes 100
  249.8 28.8 %copy-start.7 = (bf16[512,1536]{1,0:T(8,128)(2,1)S(1)}, bf16[512,1536]{1,0:T(8,128)(2,1)}, u32[]{:S(2)}) copy-start(bf16[512,1536]{1,0:T(8,128)(2,1)} %param.15) | copy-start | bytes 4718596
  249.8 802.1 %all-to-all-start.2 = ((bf16[8,256,17920]{2,1,0:T(8,128)(2,1)}), bf16[8,256,17920]{2,1,0:T(8,128)(2,1)}, u32[]{:S(2)}, u32[]{:S(2)}) async-start(bf16[8,256,17920]{2,1,0:T(8,128)(2,1)} %bitcast.18), calls=%async_computation.2 | async-start | bytes 146800640 | tf_op jit(solution)/shard_map/all_to_all | solution.py:50
  278.6 816.5 %copy-start.19 = (pred[512]{0:T(512)(128)(4,1)}, pred[512]{0:T(512)(128)(4,1)S(1)}, u32[]{:S(2)}) copy-start(pred[512]{0:T(512)(128)(4,1)S(1)} %get-tuple-element.11) | copy-start | bytes 1540
  278.6 773.3 %copy-start.17 = (s32[1024]{0:T(1024)}, s32[1024]{0:T(1024)S(1)}, u32[]{:S(2)}) copy-start(s32[1024]{0:T(1024)S(1)} %pad_clamp_fusion) | copy-start | bytes 12292
  1111.3 34.1 %copy-start.10 = (s32[2048]{0:T(1024)S(1)}, s32[2048]{0:T(1024)}, u32[]{:S(2)}) copy-start(s32[2048]{0:T(1024)} %copy-done.9) | copy-start | bytes 24580
  1145.4 63.8 %copy-start.14 = (pred[8,256]{1,0:T(8,128)(4,1)S(1)}, pred[8,256]{1,0:T(8,128)(4,1)}, u32[]{:S(2)}) copy-start(pred[8,256]{1,0:T(8,128)(4,1)} %copy-done.13) | copy-start | bytes 6148
  1233.7 410.2 %copy-start.16 = (bf16[2048,4]{0,1:T(4,128)(2,1)S(1)}, bf16[2048,4]{0,1:T(4,128)(2,1)}, u32[]{:S(2)}) copy-start(bf16[2048,4]{0,1:T(4,128)(2,1)} %copy-done.15) | copy-start | bytes 49156
  1675.2 77.5 %copy-start.18 = (s32[1024]{0:T(1024)S(1)}, s32[1024]{0:T(1024)}, u32[]{:S(2)}) copy-start(s32[1024]{0:T(1024)} %copy-done.17) | copy-start | bytes 12292
  1752.6 8.1 copy-start.8
  1752.6 8.1 copy-start.20
where the time goes:
time: 1790 us; the launch traced here: 1780 us
  waiting for transfers between devices  820 us (46%)
  blocking collectives  488 us (27%)
  matrix products  178 us (10%)
  local copies, waits for them, and re-layouts  160 us (9%)
  other arithmetic  114 us (6%)
  starting transfers between devices  22.8 us (1%)
    all_to_all x1, waiting for transfers between devices, local_step(): lax.all_to_all(gu_delta, 'ad', 0, 0, tiled=True)  750 us
    all_to_all x1, blocking collectives, local_step(): lax.all_to_all(jnp.take(hidden, send_rows, axis=0), 'ad', 0, 0, tiled=True)  410 us
    dot_general x3, matrix products, low_rank(): jnp.einsum('mar,arn->mn', low_proj, b_mat, preferred_element_type=jnp.flo...  86 us
    all_to_all x1, blocking collectives, local_step(): lax.all_to_all(low_rank(h_recv, a_down, b_down), 'ad', 0, 0, tiled=True)  77.5 us
    all_to_all x1, waiting for transfers between devices, local_step(): lax.all_to_all(jnp.take(x_rows, send_rows, axis=0), 'ad', 0, 0, tiled=True)  70.5 us
    gather x1, local copies, waits for them, and re-layouts, local_step(): jnp.take(hidden, send_rows, axis=0)  63.8 us
    concatenate x1, other arithmetic, local_step(): jnp.concatenate([low_rank(x_recv, a_gate, b_gate), low_rank(x_recv, a_up,...  48.5 us
    gather x1, local copies, waits for them, and re-layouts, local_step(): jnp.take(lax.all_to_all(gu_delta, 'ad', 0, 0, tiled=True), token_slot, ax...  43.2 us
  transfers between devices with their start and end apart: 3, of which 2 were waited for; matrix products, arithmetic and copies ran while one was open for 3% of the time, Pallas kernels for 0%

commit v1 on v0

v1 whole, which is shorter than its diff:
```python
import functools

import jax
import jax.numpy as jnp
from jax import lax
from jax.experimental import pallas as pl
from jax.experimental.pallas import tpu as pltpu
from jax.sharding import PartitionSpec as P

LORA_ALPHA = 32
PHASES = 2
LANES = 128
TILE = 128
PASS_TILES = 8
BLOCK = 256
F_BLOCK = 1280


def owner_mlp(first_ref, pool_hbm, wg_hbm, wu_hbm, wd_hbm, ag_hbm, bg_hbm, au_hbm, bu_hbm, ad_hbm, bd_hbm, out_hbm,
              starts, pool, slots, x_own, low_g, low_u, acc, acc_low, ag, au, bd, wg, wu, wd, bg, bu, ad, stage,
              pool_sem, fixed_sem, stream_sem, stage_sem, *, scale):
    n_local, d_model, rank = ag.shape
    n_blocks = pool.shape[0] // BLOCK
    n_steps = wg_hbm.shape[1] // F_BLOCK
    cap = PASS_TILES * TILE
    first = first_ref[0].astype(jnp.float32)

    def tile_rows(t):
        return pl.ds(pl.multiple_of(t * TILE, TILE), TILE)

    def block_rows(b):
        return pl.ds(pl.multiple_of(b * BLOCK, BLOCK), BLOCK)

    def load_block(b):
        return pltpu.make_async_copy(pool_hbm.at[block_rows(b), :], pool.at[block_rows(b), :], pool_sem.at[b])

    fixed = [pltpu.make_async_copy(src, dst, fixed_sem.at[i])
             for i, (src, dst) in enumerate(((ag_hbm, ag), (au_hbm, au), (bd_hbm, bd)))]

    def stream(f, s):
        cols = pl.ds(pl.multiple_of(f * F_BLOCK, F_BLOCK), F_BLOCK)
        pairs = ((wg_hbm.at[:, cols], wg), (wu_hbm.at[:, cols], wu), (bg_hbm.at[:, cols], bg),
                 (bu_hbm.at[:, cols], bu), (wd_hbm.at[cols, :], wd), (ad_hbm.at[:, cols, :], ad))
        return [pltpu.make_async_copy(src, dst.at[s], stream_sem.at[s, i]) for i, (src, dst) in enumerate(pairs)]

    def delta(wide):
        return (scale * wide).astype(jnp.bfloat16).astype(jnp.float32)

    for b in range(n_blocks):
        load_block(b).start()
    for copy in fixed:
        copy.start()
    for copy in stream(0, 0):
        copy.start()

    starts[0] = 0
    row = lax.broadcasted_iota(jnp.int32, (BLOCK, BLOCK), 0)
    col = lax.broadcasted_iota(jnp.int32, (BLOCK, BLOCK), 1)
    below = jnp.where(row >= col, 1.0, 0.0).astype(jnp.bfloat16)

    def number(b, c):
        load_block(b).wait()
        local = pool[block_rows(b), d_model:].astype(jnp.float32) - first
        mine = (local >= 0.0) & (local < n_local)
        ones = jnp.where(mine, 1.0, 0.0)
        upto = jnp.dot(below, ones.astype(jnp.bfloat16), preferred_element_type=jnp.float32)
        before = starts[b]
        slots[block_rows(b), :] = jnp.where(mine, upto + (before - 1).astype(jnp.float32), -1.0)
        starts[b + 1] = before + jnp.max(upto).astype(jnp.int32)
        return c

    lax.fori_loop(0, n_blocks, number, 0)
    owned = starts[n_blocks]
    passes = jnp.maximum(pl.cdiv(owned, cap), 1)

    def one_pass(p, carry):
        base = p * cap
        tiles = jnp.minimum(pl.cdiv(jnp.maximum(owned - base, 0), TILE), PASS_TILES)

        def pick(t, b):
            lane = lax.broadcasted_iota(jnp.int32, (BLOCK, LANES), 1) + (base + t * TILE)
            slot = slots[block_rows(b), :]
            hits = [jnp.where(slot == (lane + k).astype(jnp.float32), 1.0, 0.0) for k in range(0, TILE, LANES)]
            return jnp.concatenate(hits, axis=1).astype(jnp.bfloat16)

        @pl.when(p > 0)
        def _():
            for copy in stream(0, 0):
                copy.start()

        def clear(t, c):
            x_own[tile_rows(t), :] = jnp.zeros((TILE, x_own.shape[1]), x_own.dtype)
            acc[tile_rows(t), :] = jnp.zeros((TILE, acc.shape[1]), jnp.float32)
            acc_low[tile_rows(t), :] = jnp.zeros((TILE, acc_low.shape[1]), jnp.float32)
            return c

        lax.fori_loop(0, tiles, clear, 0)

        def gather(b, c):
            def to_tile(t, d):
                at = base + t * TILE

                @pl.when((starts[b] < at + TILE) & (starts[b + 1] > at))
                def _():
                    rows = lax.dot_general(pick(t, b), pool[block_rows(b), :], (((0,), (0,)), ((), ())),
                                           preferred_element_type=jnp.float32)
                    x_own[tile_rows(t), :] += rows.astype(x_own.dtype)
                return d

            return lax.fori_loop(0, tiles, to_tile, c)

        lax.fori_loop(0, n_blocks, gather, 0)

        @pl.when(p == 0)
        def _():
            for copy in fixed:
                copy.wait()

        def keep(t, a, wide):
            which = x_own[tile_rows(t), d_model:].astype(jnp.float32) - first
            return jnp.where(which == a, wide, 0.0)

        def project(t, c):
            rows = tile_rows(t)
            for a_mat, low in ((ag, low_g), (au, low_u)):
                for a in range(n_local):
                    proj = jnp.dot(x_own[rows, :d_model], a_mat[a], preferred_element_type=jnp.float32)
                    low[rows, a * rank:(a + 1) * rank] = keep(t, a, proj).astype(low.dtype)
            return c

        lax.fori_loop(0, tiles, project, 0)

        def hidden_block(f, c):
            s = lax.rem(f, 2)

            @pl.when(f + 1 < n_steps)
            def _():
                for copy in stream(f + 1, 1 - s):
                    copy.start()

            for copy in stream(f, s):
                copy.wait()

            def mlp(t, d):
                rows = tile_rows(t)
                x = x_own[rows, :d_model]
                gate = jnp.dot(x, wg[s], preferred_element_type=jnp.float32)
                gate += delta(jnp.dot(low_g[rows, :], bg[s], preferred_element_type=jnp.float32))
                up = jnp.dot(x, wu[s], preferred_element_type=jnp.float32)
                up += delta(jnp.dot(low_u[rows, :], bu[s], preferred_element_type=jnp.float32))
                hidden = (jax.nn.silu(gate) * up).astype(jnp.bfloat16)
                acc[rows, :] += jnp.dot(hidden, wd[s], preferred_element_type=jnp.float32)
                a_cat = jnp.concatenate([ad[s, a] for a in range(n_local)], axis=1)
                acc_low[rows, :] += jnp.dot(hidden, a_cat, preferred_element_type=jnp.float32)
                return d

            return lax.fori_loop(0, tiles, mlp, c)

        lax.fori_loop(0, n_steps, hidden_block, 0)

        def finish(t, c):
            rows = tile_rows(t)
            for a in range(n_local):
                cols = slice(a * rank, (a + 1) * rank)
                low_g[rows, cols] = keep(t, a, acc_low[rows, cols]).astype(low_g.dtype)
            y = acc[rows, :] + delta(jnp.dot(low_g[rows, :], bd[...], preferred_element_type=jnp.float32))
            x_own[rows, :d_model] = (x_own[rows, :d_model].astype(jnp.float32) + y).astype(x_own.dtype)
            return c

        lax.fori_loop(0, tiles, finish, 0)

        def flush(b, s):
            return pltpu.make_async_copy(stage.at[s], out_hbm.at[block_rows(b), :], stage_sem.at[s])

        def scatter(b, sent):
            lo, hi = starts[b], starts[b + 1]
            mine = ((hi > base) | (p == 0)) & ((lo < base + cap) | (p == passes - 1))

            @pl.when(mine)
            def _():
                s = lax.rem(sent, 2)

                @pl.when(sent >= 2)
                def _():
                    flush(b, s).wait()

                @pl.when((p > 0) & (lo < base))
                def _():
                    back = pltpu.make_async_copy(out_hbm.at[block_rows(b), :], stage.at[s], stage_sem.at[s])
                    back.start()
                    back.wait()

                @pl.when((p == 0) | (lo >= base))
                def _():
                    stage[s] = jnp.zeros(stage.shape[1:], stage.dtype)

                def from_tile(t, d):
                    at = base + t * TILE

                    @pl.when((lo < at + TILE) & (hi > at))
                    def _():
                        moved = jnp.dot(pick(t, b), x_own[tile_rows(t), :d_model], preferred_element_type=jnp.float32)
                        stage[s] += moved.astype(stage.dtype)
                    return d

                lax.fori_loop(0, tiles, from_tile, 0)
                flush(b, s).start()
            return sent + mine.astype(jnp.int32)

        sent = lax.fori_loop(0, n_blocks, scatter, jnp.int32(0))

        @pl.when(sent >= 1)
        def _():
            flush(0, lax.rem(sent + 1, 2)).wait()

        @pl.when(sent >= 2)
        def _():
            flush(0, lax.rem(sent, 2)).wait()

        return carry

    lax.fori_loop(0, passes, one_pass, 0)


def run_owner(pool, first, w_gate, w_up, w_down, a_gate, b_gate, a_up, b_up, a_down, b_down):
    n_pool, width = pool.shape
    n_local, d_model, rank = a_gate.shape
    d_ff = w_gate.shape[1]
    n_blocks = n_pool // BLOCK
    wide = n_local * rank
    cap = PASS_TILES * TILE
    hbm = pl.BlockSpec(memory_space=pl.ANY)
    flops = 2 * 384 * (3 * d_model * d_ff + 3 * wide * d_ff + 3 * wide * d_model)
    bf16, f32 = jnp.bfloat16, jnp.float32
    return pl.pallas_call(
        functools.partial(owner_mlp, scale=LORA_ALPHA / rank),
        out_shape=jax.ShapeDtypeStruct((n_pool, d_model), pool.dtype),
        in_specs=[pl.BlockSpec(memory_space=pltpu.SMEM)] + [hbm] * 10,
        out_specs=hbm,
        scratch_shapes=[
            pltpu.SMEM((n_blocks + 1,), jnp.int32),
            pltpu.VMEM((n_pool, width), bf16),
            pltpu.VMEM((n_pool, LANES), f32),
            pltpu.VMEM((cap, width), bf16),
            pltpu.VMEM((cap, wide), bf16),
            pltpu.VMEM((cap, wide), bf16),
            pltpu.VMEM((cap, d_model), f32),
            pltpu.VMEM((cap, wide), f32),
            pltpu.VMEM(a_gate.shape, bf16),
            pltpu.VMEM(a_up.shape, bf16),
            pltpu.VMEM((wide, d_model), bf16),
            pltpu.VMEM((2, d_model, F_BLOCK), bf16),
            pltpu.VMEM((2, d_model, F_BLOCK), bf16),
            pltpu.VMEM((2, F_BLOCK, d_model), bf16),
            pltpu.VMEM((2, wide, F_BLOCK), bf16),
            pltpu.VMEM((2, wide, F_BLOCK), bf16),
            pltpu.VMEM((2, n_local, F_BLOCK, rank), bf16),
            pltpu.VMEM((2, BLOCK, d_model), bf16),
            pltpu.SemaphoreType.DMA((n_blocks,)),
            pltpu.SemaphoreType.DMA((3,)),
            pltpu.SemaphoreType.DMA((2, 6)),
            pltpu.SemaphoreType.DMA((2,)),
        ],
        compiler_params=pltpu.CompilerParams(vmem_limit_bytes=67043328),
        cost_estimate=pl.CostEstimate(flops=flops, bytes_accessed=140_000_000, transcendentals=0),
    )(first, pool, w_gate, w_up, w_down, a_gate, b_gate.reshape(wide, d_ff), a_up, b_up.reshape(wide, d_ff),
      a_down, b_down.reshape(wide, d_model))


def spread_order(adapter_id, parts):
    n_rows = adapter_id.shape[0]
    index = jnp.arange(n_rows)
    ahead = (adapter_id[None, :] < adapter_id[:, None]) | (
        (adapter_id[None, :] == adapter_id[:, None]) & (index[None, :] < index[:, None]))
    rank = jnp.sum(ahead.astype(jnp.int32), axis=1)
    return (rank % parts) * (n_rows // parts) + rank // parts


def solution(mesh):
    n_dp = mesh.shape["dp"]
    tok_axes = ("rep", "dp", "ad")
    row_spec = P(tok_axes, None)
    owned = P("ad", None, None)

    def local_step(x_rows, adapter_id, *weights):
        n_rows, d_model = x_rows.shape
        n_local = weights[3].shape[0]
        part = n_rows // (PHASES * n_dp)
        dest = spread_order(adapter_id, PHASES * n_dp)
        move = (dest[None, :] == jnp.arange(n_rows)[:, None]).astype(jnp.bfloat16)
        tagged = jnp.concatenate(
            [x_rows, jnp.broadcast_to(adapter_id.astype(x_rows.dtype)[:, None], (n_rows, LANES))], axis=1)
        tagged = jnp.dot(move, tagged, preferred_element_type=jnp.float32).astype(x_rows.dtype)
        tagged = tagged.reshape(PHASES, n_dp, part, d_model + LANES)
        first = (lax.axis_index("ad") * n_local).astype(jnp.int32).reshape(1)
        back = []
        spread = [lax.all_to_all(tagged[ph], "dp", 0, 0) for ph in range(PHASES)]
        pools = [lax.all_gather(s.reshape(n_dp * part, -1), "ad", axis=0, tiled=True) for s in spread]
        done = [run_owner(pool, first, *weights) for pool in pools]
        for d in done:
            mine = lax.psum_scatter(d, "ad", scatter_dimension=0, tiled=True)
            back.append(lax.all_to_all(mine.reshape(n_dp, part, d_model), "dp", 0, 0))
        back = jnp.stack(back).reshape(n_rows, d_model)
        return jnp.dot(move.T, back, preferred_element_type=jnp.float32).astype(x_rows.dtype)

    return jax.shard_map(local_step, mesh=mesh,
                         in_specs=(row_spec, P(tok_axes), P(), P(), P(), owned, owned, owned, owned, owned, owned),
                         out_specs=row_spec, check_vma=False)
```

time: 1790 us -> 277 us (0.15)
  waiting for transfers between devices: 820 us -> 91.1 us
  blocking collectives: 488 us -> 51.9 us
  matrix products: 178 us -> 4.73 us
  local copies, waits for them, and re-layouts: 160 us -> 0.79 us
  other arithmetic: 114 us -> 1.92 us
  Pallas kernels: 0 us -> 105 us
    all_to_all x3 -> x1, waiting for transfers between devices: 820 us -> 0.01 us  [local_step(): back.append(lax.all_to_all(mine.reshape(n_dp, part, d_model), 'dp', 0, 0))]
    all_to_all x2 -> x3, blocking collectives: 488 us -> 51.9 us  [the longest x2 34.1 us: local_step(): spread = [lax.all_to_all(tagged[ph], 'dp', 0, 0) for ph in range(PHASES)]]
    dot_general x8 -> x2, matrix products: 178 us -> 4.73 us  [the longest x1 2.54 us: local_step(): jnp.dot(move, tagged, preferred_element_type=jnp.float32)]
    gather x9 -> x0, local copies, waits for them, and re-layouts: 159 us -> none  [the longest x1 63.8 us: local_step(): jnp.take(hidden, send_rows, axis=0)]
    pallas_call x0 -> x2, Pallas kernels: none -> 105 us  [run_owner(): pl.pallas_call(functools.partial(owner_mlp, scale=LORA_ALPHA / rank), out...]
    reduce_scatter x0 -> x2, waiting for transfers between devices: none -> 67.3 us  [local_step(): mine = lax.psum_scatter(d, 'ad', scatter_dimension=0, tiled=True)]
    concatenate x1 -> x0, other arithmetic: 48.5 us -> none  [local_step(): jnp.concatenate([low_rank(x_recv, a_gate, b_gate), low_rank(x_recv, a_up,...]
    select_n x6 -> x0, other arithmetic: 47.5 us -> none  [the longest x1 24.5 us: local_step(): jnp.take(hidden, send_rows, axis=0)]
  transfers between devices with their start and end apart: 3 -> 5, of which waited for: 2 -> 3; matrix products, arithmetic and copies ran while one was open for 3% -> 0% of each run, Pallas kernels for 0% -> 38%
where the time goes in v1:
time: 277 us
  Pallas kernels  105 us (38%)
  waiting for transfers between devices  91.1 us (33%)
  blocking collectives  51.9 us (19%)
  between operations  13.2 us (5%)
  starting transfers between devices  7.45 us (3%)
  matrix products  4.73 us (2%)
    pallas_call x2, Pallas kernels, run_owner(): pl.pallas_call(functools.partial(owner_mlp, scale=LORA_ALPHA / rank), out...  105 us
    reduce_scatter x2, waiting for transfers between devices, local_step(): mine = lax.psum_scatter(d, 'ad', scatter_dimension=0, tiled=True)  67.3 us
    all_to_all x2, blocking collectives, local_step(): spread = [lax.all_to_all(tagged[ph], 'dp', 0, 0) for ph in range(PHASES)]  34.1 us
    all_gather x2, waiting for transfers between devices, local_step(): lax.all_gather(s.reshape(n_dp * part, -1), 'ad', axis=0, tiled=True)  23.6 us
    all_to_all x1, blocking collectives, local_step(): back.append(lax.all_to_all(mine.reshape(n_dp, part, d_model), 'dp', 0, 0))  17.7 us
    all_to_all x1, starting transfers between devices, local_step(): back.append(lax.all_to_all(mine.reshape(n_dp, part, d_model), 'dp', 0, 0))  7.26 us
  transfers between devices with their start and end apart: 5, of which 3 were waited for; matrix products, arithmetic and copies ran while one was open for 0% of the time, Pallas kernels for 38%

profile of v1, /device:TPU:98, one launch (start us, length us, event | category | flops | bytes accessed | tf_op | source)
XLA Modules:
  0.0 276.6 jit_solution(17992358160172293193)
XLA Ops:
  6.5 0.0 all-gather.5.cloned.1.call-start
  6.6 0.7 convert_element_type.14
  7.2 1.1 convert_reduce_fusion
  8.3 0.0 copy-start
  8.3 0.1 broadcast_in_dim.2
  8.5 2.5 convolution_convert_fusion.1
  11.0 0.0 copy-done
  11.0 0.1 fusion.12
  11.2 18.8 %all_to_all.20 = bf16[4,64,1664]{2,1,0:T(8,128)(2,1)} all-to-all(bf16[4,64,1664]{2,1,0:T(8,128)(2,1)S(1)} %bitcast.17), channel_id=1, replica_groups=mesh['rep'=1,'dp'=4,'ad'=8] {'dp'}, dimensions={0} | all-to-all | bytes 1703936 | tf_op jit(solution)/shard_map/all_to_all | solution.py:297
  30.0 0.1 all-gather.5.cloned.1.call-update
  30.0 0.1 all-gather.3.cloned.1.call-start
  30.1 15.4 %all_to_all.21 = bf16[4,64,1664]{2,1,0:T(8,128)(2,1)} all-to-all(bf16[4,64,1664]{2,1,0:T(8,128)(2,1)S(1)} %bitcast.16), channel_id=1, replica_groups=mesh['rep'=1,'dp'=4,'ad'=8] {'dp'}, dimensions={0} | all-to-all | bytes 1703936 | tf_op jit(solution)/shard_map/all_to_all | solution.py:297
  45.5 0.1 all-gather.3.cloned.1.call-update
  45.5 0.1 reduce-scatter.5.cloned.1.call-start
  45.6 23.6 %all-gather.5.cloned.1.call-done.pool_hbm = bf16[2048,1664]{1,0:T(8,128)(2,1)} async-done(((bf16[256,1664]{1,0:T(8,128)(2,1)}), bf16[2048,1664]{1,0:T(8,128)(2,1)}) %all-gather.5.cloned.1.call-update) | async-done | bytes 6815760 | tf_op jit(solution)/shard_map/all_gather | solution.py:298
  69.2 56.2 %shard_map.110 = bf16[2048,1536]{1,0:T(8,128)(2,1)} custom-call(s32[1]{0:T(128)} %bitcast.first_ref, bf16[2048,1664]{1,0:T(8,128)(2,1)} %all-gather.5.cloned.1.call-done.pool_hbm, bf16[1536,8960]{1,0:T(8,128)(2,1)} %wg_hbm.3, bf16[1536,8960]{1,0:T(8,128)(2,1)} %wu_hbm.3, bf16[8960,1536]{1,0:T(8,128)(2,1)} %wd_hbm.3, bf16[4,1536,128]{2,1,0:T(8,128)(2,1)} %ag_hbm.3, ...), custom_call_target="tpu_custom_call" | custom-call | flops 44090523648 | bytes 140000000 | tf_op jit(solution)/shard_map/pallas_call | solution.py:235
  125.4 0.1 reduce-scatter.5.cloned.1.call-update
  125.5 0.1 reduce-scatter.3.cloned.1.call-start
  125.5 0.0 all-gather.3.cloned.1.call-done.pool_hbm
  125.6 49.2 %shard_map.109 = bf16[2048,1536]{1,0:T(8,128)(2,1)} custom-call(s32[1]{0:T(128)} %bitcast.first_ref, bf16[2048,1664]{1,0:T(8,128)(2,1)} %all-gather.3.cloned.1.call-done.pool_hbm, bf16[1536,8960]{1,0:T(8,128)(2,1)} %wg_hbm.3, bf16[1536,8960]{1,0:T(8,128)(2,1)} %wu_hbm.3, bf16[8960,1536]{1,0:T(8,128)(2,1)} %wd_hbm.3, bf16[4,1536,128]{2,1,0:T(8,128)(2,1)} %ag_hbm.3, ...), custom_call_target="tpu_custom_call" | custom-call | flops 44090523648 | bytes 140000000 | tf_op jit(solution)/shard_map/pallas_call | solution.py:235
  174.8 0.1 reduce-scatter.3.cloned.1.call-update
  174.9 4.0 %reduce-scatter.5.cloned.1.call-done = bf16[256,1536]{1,0:T(8,128)(2,1)} async-done(((bf16[2048,1536]{1,0:T(8,128)(2,1)}), bf16[256,1536]{1,0:T(8,128)(2,1)}) %reduce-scatter.5.cloned.1.call-update) | async-done | bytes 786448 | tf_op jit(solution)/shard_map/reduce_scatter | solution.py:301
  178.9 7.3 %all-to-all-start.3 = ((bf16[4,64,1536]{2,1,0:T(8,128)(2,1)}), bf16[4,64,1536]{2,1,0:T(8,128)(2,1)S(1)}, u32[]{:S(2)}, u32[]{:S(2)}) async-start(bf16[4,64,1536]{2,1,0:T(8,128)(2,1)} %bitcast.21), calls=%async_computation.5 | async-start | bytes 1572864 | tf_op jit(solution)/shard_map/all_to_all | solution.py:302
  186.1 63.3 %reduce-scatter.3.cloned.1.call-done = bf16[256,1536]{1,0:T(8,128)(2,1)} async-done(((bf16[2048,1536]{1,0:T(8,128)(2,1)}), bf16[256,1536]{1,0:T(8,128)(2,1)}) %reduce-scatter.3.cloned.1.call-update) | async-done | bytes 786448 | tf_op jit(solution)/shard_map/reduce_scatter | solution.py:301
  249.4 0.0 all-to-all-done.3
  249.4 17.7 %all_to_all.22 = bf16[4,64,1536]{2,1,0:T(8,128)(2,1)S(1)} all-to-all(bf16[4,64,1536]{2,1,0:T(8,128)(2,1)} %bitcast.22), channel_id=1, replica_groups=mesh['rep'=1,'dp'=4,'ad'=8] {'dp'}, dimensions={0} | all-to-all | bytes 1572864 | tf_op jit(solution)/shard_map/all_to_all | solution.py:302
  267.1 0.0 copy-start.1
  267.1 0.1 pad_maximum_fusion
  267.3 0.5 copy-done.1
  267.8 2.2 convolution_convert_fusion
  (1 shorter events, 0.0 us)
Async XLA Ops:
  6.5 62.7 %all-gather.5.cloned.1.call-start = ((), (), s32[]{:S(2)}) async-start(), calls=%async_computation.8 | async-start | bytes 7667712 | tf_op jit(solution)/shard_map/all_gather | solution.py:298
  8.3 2.7 copy-start
  30.0 95.5 %all-gather.3.cloned.1.call-start = ((), (), s32[]{:S(2)}) async-start(), calls=%async_computation.6 | async-start | bytes 7667712 | tf_op jit(solution)/shard_map/all_gather | solution.py:298
  45.5 133.3 %reduce-scatter.5.cloned.1.call-start = ((), (), s32[]{:S(2)}) async-start(), calls=%async_computation.9 | async-start | bytes 7077888 | tf_op jit(solution)/shard_map/reduce_scatter | solution.py:301
  125.5 123.9 %reduce-scatter.3.cloned.1.call-start = ((), (), s32[]{:S(2)}) async-start(), calls=%async_computation.7 | async-start | bytes 7077888 | tf_op jit(solution)/shard_map/reduce_scatter | solution.py:301
  178.9 70.6 %all-to-all-start.3 = ((bf16[4,64,1536]{2,1,0:T(8,128)(2,1)}), bf16[4,64,1536]{2,1,0:T(8,128)(2,1)S(1)}, u32[]{:S(2)}, u32[]{:S(2)}) async-start(bf16[4,64,1536]{2,1,0:T(8,128)(2,1)} %bitcast.21), calls=%async_computation.5 | async-start | bytes 1572864 | tf_op jit(solution)/shard_map/all_to_all | solution.py:302
  267.1 0.7 copy-start.1
Sparse Core Ops, SparseCore 0:
  30.1 39.0 all-gather.4
  70.8 40.4 all-gather.2
  125.6 53.2 reduce-scatter.4
  181.0 68.3 reduce-scatter.2

commit v2 on v1

v2 whole, which is shorter than its diff:
```python
import functools

import jax
import jax.numpy as jnp
from jax import lax
from jax.experimental import pallas as pl
from jax.experimental.pallas import tpu as pltpu
from jax.sharding import PartitionSpec as P

LORA_ALPHA = 32
PHASES = 2
LANES = 128
TILE = 192
MIN_TILES = 2
MAX_TILES = 4
PACK = 256
BLOCK = 256
F_BLOCK = 1280


def owner_mlp(first_ref, pool_hbm, wg_hbm, wu_hbm, wd_hbm, ag_hbm, bg_hbm, au_hbm, bu_hbm, ad_hbm, bd_hbm, out_hbm,
              pool, relative, slots, pick, x_own, low, acc, acc_low, a_in, bd, wg, wu, wd, bg, bu, ad, stage, hidden,
              pool_sem, fixed_sem, stream_sem, stage_sem, *, scale, n_local, rank):
    n_groups, depth, d_model = bd.shape
    per_group = n_local // n_groups
    n_blocks = pool.shape[0] // BLOCK
    n_steps = wg_hbm.shape[1] // F_BLOCK
    first = first_ref[0].astype(jnp.float32)
    f32, bf16 = jnp.float32, jnp.bfloat16

    def block_rows(b):
        return pl.ds(b * BLOCK, BLOCK)

    def tile_rows(t):
        return pl.ds(pl.multiple_of(t * TILE, TILE), TILE)

    def load_block(b):
        return pltpu.make_async_copy(pool_hbm.at[block_rows(b), :], pool.at[block_rows(b), :], pool_sem.at[b])

    fixed = [pltpu.make_async_copy(bd_hbm, bd, fixed_sem.at[0])]
    for k, src in enumerate((ag_hbm, au_hbm)):
        for a in range(n_local):
            dst = a_in.at[a // per_group, :, pl.ds(k * depth + a % per_group * rank, rank)]
            fixed.append(pltpu.make_async_copy(src.at[a], dst, fixed_sem.at[1 + k * n_local + a]))

    def stream(f, s):
        cols = pl.ds(pl.multiple_of(f * F_BLOCK, F_BLOCK), F_BLOCK)
        pairs = [(wg_hbm.at[:, cols], wg.at[s]), (bg_hbm.at[:, :, cols], bg.at[s]),
                 (wu_hbm.at[:, cols], wu.at[s]), (bu_hbm.at[:, :, cols], bu.at[s]), (wd_hbm.at[cols, :], wd.at[s])]
        pairs += [(ad_hbm.at[a, cols, :], ad.at[s, a // per_group, :, pl.ds(a % per_group * rank, rank)])
                  for a in range(n_local)]
        return [pltpu.make_async_copy(src, dst, stream_sem.at[s, i]) for i, (src, dst) in enumerate(pairs)]

    def delta(product):
        return (scale * product).astype(bf16).astype(f32)

    for b in range(n_blocks):
        load_block(b).start()
    lane = jnp.where(lax.broadcasted_iota(jnp.int32, (8, LANES), 1) == 0, 1.0, 0.0).astype(bf16)
    upper = jnp.where(lax.broadcasted_iota(jnp.int32, (BLOCK, BLOCK), 0)
                      <= lax.broadcasted_iota(jnp.int32, (BLOCK, BLOCK), 1), 1.0, 0.0).astype(bf16)
    group = lax.broadcasted_iota(jnp.int32, (8, BLOCK), 0)
    lowest = (group * per_group).astype(f32)
    before = jnp.zeros((8, BLOCK), f32)
    for b in range(n_blocks):
        load_block(b).wait()
    for copy in fixed:
        copy.start()
    for copy in stream(0, 0):
        copy.start()
    for b in range(n_blocks):
        ids = lax.dot_general(lane, pool[block_rows(b), d_model:], (((1,), (1,)), ((), ())), preferred_element_type=f32)
        local = ids - first - lowest
        mine = (local >= 0.0) & (local < per_group) & (group < n_groups)
        upto = jnp.dot(jnp.where(mine, 1.0, 0.0).astype(bf16), upper, preferred_element_type=f32)
        place = jnp.where(mine, upto + (before - 1.0), -1e6)
        for g in range(n_groups):
            relative[g, b:b + 1, :] = place[g:g + 1, :]
        before = before + jnp.broadcast_to(upto[:, BLOCK - 1:], (8, BLOCK))
    begins = [jnp.int32(0)]
    for g in range(n_groups):
        begins.append(begins[-1] + pl.cdiv(jnp.max(before[g:g + 1, :]).astype(jnp.int32), TILE))
    slot = relative[0]
    for g in range(1, n_groups):
        slot = jnp.maximum(slot, relative[g] + (begins[g] * TILE).astype(f32))
    slots[...] = slot
    passes = jnp.maximum(pl.cdiv(begins[-1], MAX_TILES), 1)

    def one_pass(p, carry):
        tiles = jnp.where(begins[-1] - p * MAX_TILES > MIN_TILES, MAX_TILES, MIN_TILES)

        def group_of(t):
            at = t + p * MAX_TILES
            return sum([(at >= begins[g]).astype(jnp.int32) for g in range(1, n_groups)], jnp.int32(0))

        @pl.when(p > 0)
        def _():
            for copy in stream(0, 0):
                copy.start()

        def gather(t, c):
            rows = tile_rows(t)
            target = (lax.broadcasted_iota(jnp.int32, (TILE, BLOCK), 0) + (p * MAX_TILES + t) * TILE).astype(f32)
            for b in range(n_blocks):
                hit = jnp.broadcast_to(slots[b:b + 1, :], (TILE, BLOCK)) == target
                pick[rows, b * BLOCK:(b + 1) * BLOCK] = jnp.where(hit, 1.0, 0.0).astype(bf16)
            x_own[rows, :] = jnp.dot(pick[rows, :], pool[...], preferred_element_type=f32).astype(bf16)
            acc[rows, :] = jnp.zeros((TILE, d_model), f32)
            acc_low[rows, :] = jnp.zeros((TILE, depth), f32)
            return c

        lax.fori_loop(0, tiles, gather, 0)

        @pl.when(p == 0)
        def _():
            for copy in fixed:
                copy.wait()

        def keep(t, product):
            which = x_own[tile_rows(t), d_model:].astype(f32) - first - (group_of(t) * per_group).astype(f32)
            parts = [jnp.where(which == a, product[:, a * rank:(a + 1) * rank], 0.0) for a in range(per_group)]
            return jnp.concatenate(parts, axis=1).astype(bf16)

        def project(t, c):
            rows = tile_rows(t)
            proj = jnp.dot(x_own[rows, :d_model], a_in[group_of(t)], preferred_element_type=f32)
            for k in range(2):
                low[k, rows, :] = keep(t, proj[:, k * depth:(k + 1) * depth])
            return c

        lax.fori_loop(0, tiles, project, 0)

        def hidden_block(f, c):
            s = lax.rem(f, 2)

            @pl.when(f + 1 < n_steps)
            def _():
                for copy in stream(f + 1, 1 - s):
                    copy.start()

            for copy in stream(f, s):
                copy.wait()

            def mlp(u, d):
                tiles_of = [u * MIN_TILES + k for k in range(MIN_TILES)]
                rows = pl.ds(pl.multiple_of(u * (MIN_TILES * TILE), TILE), MIN_TILES * TILE)
                x = x_own[rows, :d_model]

                def deltas(k, b_mat):
                    return jnp.concatenate([delta(jnp.dot(low[k, tile_rows(t), :], b_mat[s, group_of(t)],
                                                          preferred_element_type=f32)) for t in tiles_of], axis=0)

                gate = jnp.dot(x, wg[s], preferred_element_type=f32) + deltas(0, bg)
                up = jnp.dot(x, wu[s], preferred_element_type=f32) + deltas(1, bu)
                hidden[...] = (jax.nn.silu(gate) * up).astype(bf16)
                acc[rows, :] += jnp.dot(hidden[...], wd[s], preferred_element_type=f32)
                for k, t in enumerate(tiles_of):
                    acc_low[tile_rows(t), :] += jnp.dot(hidden[k * TILE:(k + 1) * TILE, :], ad[s, group_of(t)],
                                                        preferred_element_type=f32)
                return d

            return lax.fori_loop(0, lax.div(tiles, MIN_TILES), mlp, c)

        lax.fori_loop(0, n_steps, hidden_block, 0)

        def finish(t, c):
            rows = tile_rows(t)
            y = acc[rows, :] + delta(jnp.dot(keep(t, acc_low[rows, :]), bd[group_of(t)], preferred_element_type=f32))
            x_own[rows, :d_model] = (x_own[rows, :d_model].astype(f32) + y).astype(bf16)
            return c

        lax.fori_loop(0, tiles, finish, 0)

        def moved(n_rows, cols):
            return lax.dot_general(pick[:n_rows, cols], x_own[:n_rows, :d_model], (((0,), (0,)), ((), ())),
                                   preferred_element_type=f32).astype(bf16)

        small = (p == 0) & (tiles == MIN_TILES)

        @pl.when(small)
        def _():
            def flush(b):
                return pltpu.make_async_copy(stage.at[b % 2], out_hbm.at[block_rows(b), :], stage_sem.at[b % 2])

            for b in range(n_blocks):
                if b >= 2:
                    flush(b - 2).wait()
                stage[b % 2] = moved(MIN_TILES * TILE, block_rows(b))
                flush(b).start()
            flush(n_blocks - 2).wait()
            flush(n_blocks - 1).wait()

        @pl.when(jnp.logical_not(small))
        def _():
            def blank(t, c):
                pick[tile_rows(t), :] = jnp.zeros((TILE, pick.shape[1]), bf16)
                x_own[tile_rows(t), :] = jnp.zeros((TILE, x_own.shape[1]), bf16)
                return c

            lax.fori_loop(tiles, MAX_TILES, blank, 0)

            def block(b, c):
                at = pl.ds(pl.multiple_of(b * BLOCK, BLOCK), BLOCK)
                stage[0] = jnp.zeros(stage.shape[1:], bf16)

                @pl.when(p > 0)
                def _():
                    back = pltpu.make_async_copy(out_hbm.at[at, :], stage.at[0], stage_sem.at[0])
                    back.start()
                    back.wait()

                stage[0] = stage[0] + moved(MAX_TILES * TILE, at)
                put = pltpu.make_async_copy(stage.at[0], out_hbm.at[at, :], stage_sem.at[0])
                put.start()
                put.wait()
                return c

            lax.fori_loop(0, n_blocks, block, 0)

        return carry

    lax.fori_loop(0, passes, one_pass, 0)


def run_owner(pool, first, w_gate, w_up, w_down, a_gate, b_gate, a_up, b_up, a_down, b_down):
    n_pool, width = pool.shape
    n_local, d_model, rank = a_gate.shape
    d_ff = w_gate.shape[1]
    n_blocks = n_pool // BLOCK
    per_group = min(n_local, max(1, PACK // rank))
    n_groups, depth = n_local // per_group, per_group * rank
    rows = MAX_TILES * TILE
    hbm = pl.BlockSpec(memory_space=pl.ANY)
    flops = 2 * MIN_TILES * TILE * (3 * d_model * d_ff + 3 * depth * d_ff + 3 * depth * d_model)
    bf16, f32 = jnp.bfloat16, jnp.float32
    return pl.pallas_call(
        functools.partial(owner_mlp, scale=LORA_ALPHA / rank, n_local=n_local, rank=rank),
        out_shape=jax.ShapeDtypeStruct((n_pool, d_model), pool.dtype),
        in_specs=[pl.BlockSpec(memory_space=pltpu.SMEM)] + [hbm] * 10,
        out_specs=hbm,
        scratch_shapes=[
            pltpu.VMEM((n_pool, width), bf16),
            pltpu.VMEM((n_groups, n_blocks, BLOCK), f32),
            pltpu.VMEM((n_blocks, BLOCK), f32),
            pltpu.VMEM((rows, n_pool), bf16),
            pltpu.VMEM((rows, width), bf16),
            pltpu.VMEM((2, rows, depth), bf16),
            pltpu.VMEM((rows, d_model), f32),
            pltpu.VMEM((rows, depth), f32),
            pltpu.VMEM((n_groups, d_model, 2 * depth), bf16),
            pltpu.VMEM((n_groups, depth, d_model), bf16),
            pltpu.VMEM((2, d_model, F_BLOCK), bf16),
            pltpu.VMEM((2, d_model, F_BLOCK), bf16),
            pltpu.VMEM((2, F_BLOCK, d_model), bf16),
            pltpu.VMEM((2, n_groups, depth, F_BLOCK), bf16),
            pltpu.VMEM((2, n_groups, depth, F_BLOCK), bf16),
            pltpu.VMEM((2, n_groups, F_BLOCK, depth), bf16),
            pltpu.VMEM((2, BLOCK, d_model), bf16),
            pltpu.VMEM((MIN_TILES * TILE, F_BLOCK), bf16),
            pltpu.SemaphoreType.DMA((n_blocks,)),
            pltpu.SemaphoreType.DMA((2 * n_local + 1,)),
            pltpu.SemaphoreType.DMA((2, 5 + n_local)),
            pltpu.SemaphoreType.DMA((2,)),
        ],
        compiler_params=pltpu.CompilerParams(vmem_limit_bytes=67043328),
        cost_estimate=pl.CostEstimate(flops=flops, bytes_accessed=140_000_000, transcendentals=0),
    )(first, pool, w_gate, w_up, w_down, a_gate, b_gate.reshape(n_groups, depth, d_ff),
      a_up, b_up.reshape(n_groups, depth, d_ff), a_down, b_down.reshape(n_groups, depth, d_model))


def spread_order(adapter_id, parts):
    n_rows = adapter_id.shape[0]
    index = jnp.arange(n_rows)
    ahead = (adapter_id[None, :] < adapter_id[:, None]) | (
        (adapter_id[None, :] == adapter_id[:, None]) & (index[None, :] < index[:, None]))
    rank = jnp.sum(ahead.astype(jnp.int32), axis=1)
    return (rank % parts) * (n_rows // parts) + rank // parts


def solution(mesh):
    n_dp = mesh.shape["dp"]
    tok_axes = ("rep", "dp", "ad")
    row_spec = P(tok_axes, None)
    owned = P("ad", None, None)

    def local_step(x_rows, adapter_id, *weights):
        n_rows, d_model = x_rows.shape
        n_local = weights[3].shape[0]
        part = n_rows // (PHASES * n_dp)
        dest = spread_order(adapter_id, PHASES * n_dp)
        move = (dest[None, :] == jnp.arange(n_rows)[:, None]).astype(jnp.bfloat16)
        tagged = jnp.concatenate(
            [x_rows, jnp.broadcast_to(adapter_id.astype(x_rows.dtype)[:, None], (n_rows, LANES))], axis=1)
        tagged = jnp.dot(move, tagged, preferred_element_type=jnp.float32).astype(x_rows.dtype)
        tagged = tagged.reshape(PHASES, n_dp, part, d_model + LANES)
        first = (lax.axis_index("ad") * n_local).astype(jnp.int32).reshape(1)
        back = []
        spread = [lax.all_to_all(tagged[ph], "dp", 0, 0) for ph in range(PHASES)]
        pools = [lax.all_gather(s.reshape(n_dp * part, -1), "ad", axis=0, tiled=True) for s in spread]
        done = [run_owner(pool, first, *weights) for pool in pools]
        for d in done:
            mine = lax.psum_scatter(d, "ad", scatter_dimension=0, tiled=True)
            back.append(lax.all_to_all(mine.reshape(n_dp, part, d_model), "dp", 0, 0))
        back = jnp.stack(back).reshape(n_rows, d_model)
        return jnp.dot(move.T, back, preferred_element_type=jnp.float32).astype(x_rows.dtype)

    return jax.shard_map(local_step, mesh=mesh,
                         in_specs=(row_spec, P(tok_axes), P(), P(), P(), owned, owned, owned, owned, owned, owned),
                         out_specs=row_spec, check_vma=False)
```

time: 277 us -> 256 us (0.924)
  waiting for transfers between devices: 91.1 us -> 58.4 us
  Pallas kernels: 105 us -> 120 us
    reduce_scatter x2, waiting for transfers between devices: 67.3 us -> 34.7 us  [local_step(): mine = lax.psum_scatter(d, 'ad', scatter_dimension=0, tiled=True)]
    pallas_call x2, Pallas kernels: 105 us -> 120 us  [run_owner(): pl.pallas_call(functools.partial(owner_mlp, scale=LORA_ALPHA / rank, n_lo...]
    all_to_all x1, starting transfers between devices: 7.26 us -> 4.33 us  [local_step(): back.append(lax.all_to_all(mine.reshape(n_dp, part, d_model), 'dp', 0, 0))]
  transfers between devices with their start and end apart: 5 -> 5, of which waited for: 3 -> 2; matrix products, arithmetic and copies ran while one was open for 0% -> 0% of each run, Pallas kernels for 38% -> 47%
where the time goes in v2:
time: 256 us
  Pallas kernels  120 us (47%)
  waiting for transfers between devices  58.4 us (23%)
  blocking collectives  51.9 us (20%)
  between operations  13.2 us (5%)
  starting transfers between devices  4.93 us (2%)
  matrix products  4.72 us (2%)
    pallas_call x2, Pallas kernels, run_owner(): pl.pallas_call(functools.partial(owner_mlp, scale=LORA_ALPHA / rank, n_lo...  120 us
    reduce_scatter x2, waiting for transfers between devices, local_step(): mine = lax.psum_scatter(d, 'ad', scatter_dimension=0, tiled=True)  34.7 us
    all_to_all x2, blocking collectives, local_step(): spread = [lax.all_to_all(tagged[ph], 'dp', 0, 0) for ph in range(PHASES)]  34.2 us
    all_gather x2, waiting for transfers between devices, local_step(): lax.all_gather(s.reshape(n_dp * part, -1), 'ad', axis=0, tiled=True)  23.4 us
    all_to_all x1, blocking collectives, local_step(): back.append(lax.all_to_all(mine.reshape(n_dp, part, d_model), 'dp', 0, 0))  17.8 us
  transfers between devices with their start and end apart: 5, of which 2 were waited for; matrix products, arithmetic and copies ran while one was open for 0% of the time, Pallas kernels for 47%

profile of v2, /device:TPU:98, one launch (start us, length us, event | category | flops | bytes accessed | tf_op | source)
XLA Modules:
  0.0 255.9 jit_solution(9789945550905472527)
XLA Ops:
  6.5 0.0 all-gather.5.cloned.1.call-start
  6.6 0.7 convert_element_type.14
  7.2 1.1 convert_reduce_fusion
  8.3 0.0 copy-start
  8.3 0.1 broadcast_in_dim.2
  8.5 2.5 convolution_convert_fusion.1
  11.0 0.0 copy-done
  11.0 0.1 fusion.12
  11.2 18.8 %all_to_all.20 = bf16[4,64,1664]{2,1,0:T(8,128)(2,1)} all-to-all(bf16[4,64,1664]{2,1,0:T(8,128)(2,1)S(1)} %bitcast.17), channel_id=1, replica_groups=mesh['rep'=1,'dp'=4,'ad'=8] {'dp'}, dimensions={0} | all-to-all | bytes 1703936 | tf_op jit(solution)/shard_map/all_to_all | solution.py:298
  30.0 0.1 all-gather.5.cloned.1.call-update
  30.0 0.1 all-gather.3.cloned.1.call-start
  30.1 15.4 %all_to_all.21 = bf16[4,64,1664]{2,1,0:T(8,128)(2,1)} all-to-all(bf16[4,64,1664]{2,1,0:T(8,128)(2,1)S(1)} %bitcast.16), channel_id=1, replica_groups=mesh['rep'=1,'dp'=4,'ad'=8] {'dp'}, dimensions={0} | all-to-all | bytes 1703936 | tf_op jit(solution)/shard_map/all_to_all | solution.py:298
  45.5 0.1 all-gather.3.cloned.1.call-update
  45.5 0.2 reduce-scatter.5.cloned.1.call-start
  45.8 23.4 %all-gather.5.cloned.1.call-done.pool_hbm = bf16[2048,1664]{1,0:T(8,128)(2,1)} async-done(((bf16[256,1664]{1,0:T(8,128)(2,1)}), bf16[2048,1664]{1,0:T(8,128)(2,1)}) %all-gather.5.cloned.1.call-update) | async-done | bytes 6815760 | tf_op jit(solution)/shard_map/all_gather | solution.py:299
  69.2 60.0 %shard_map.110 = bf16[2048,1536]{1,0:T(8,128)(2,1)} custom-call(s32[1]{0:T(128)} %bitcast.first_ref, bf16[2048,1664]{1,0:T(8,128)(2,1)} %all-gather.5.cloned.1.call-done.pool_hbm, bf16[1536,8960]{1,0:T(8,128)(2,1)} %wg_hbm.3, bf16[1536,8960]{1,0:T(8,128)(2,1)} %wu_hbm.3, bf16[8960,1536]{1,0:T(8,128)(2,1)} %wd_hbm.3, bf16[4,1536,128]{2,1,0:T(8,128)(2,1)} %ag_hbm.3, ...), custom_call_target="tpu_custom_call" | custom-call | flops 37899730944 | bytes 140000000 | tf_op jit(solution)/shard_map/pallas_call | solution.py:236
  129.2 0.1 reduce-scatter.5.cloned.1.call-update
  129.2 0.3 reduce-scatter.3.cloned.1.call-start
  129.5 0.0 all-gather.3.cloned.1.call-done.pool_hbm
  129.6 60.1 %shard_map.109 = bf16[2048,1536]{1,0:T(8,128)(2,1)} custom-call(s32[1]{0:T(128)} %bitcast.first_ref, bf16[2048,1664]{1,0:T(8,128)(2,1)} %all-gather.3.cloned.1.call-done.pool_hbm, bf16[1536,8960]{1,0:T(8,128)(2,1)} %wg_hbm.3, bf16[1536,8960]{1,0:T(8,128)(2,1)} %wu_hbm.3, bf16[8960,1536]{1,0:T(8,128)(2,1)} %wd_hbm.3, bf16[4,1536,128]{2,1,0:T(8,128)(2,1)} %ag_hbm.3, ...), custom_call_target="tpu_custom_call" | custom-call | flops 37899730944 | bytes 140000000 | tf_op jit(solution)/shard_map/pallas_call | solution.py:236
  189.6 0.1 reduce-scatter.3.cloned.1.call-update
  189.7 0.0 reduce-scatter.5.cloned.1.call-done
  189.7 4.3 %all-to-all-start.3 = ((bf16[4,64,1536]{2,1,0:T(8,128)(2,1)}), bf16[4,64,1536]{2,1,0:T(8,128)(2,1)S(1)}, u32[]{:S(2)}, u32[]{:S(2)}) async-start(bf16[4,64,1536]{2,1,0:T(8,128)(2,1)} %bitcast.21), calls=%async_computation.5 | async-start | bytes 1572864 | tf_op jit(solution)/shard_map/all_to_all | solution.py:303
  194.1 34.7 %reduce-scatter.3.cloned.1.call-done = bf16[256,1536]{1,0:T(8,128)(2,1)} async-done(((bf16[2048,1536]{1,0:T(8,128)(2,1)}), bf16[256,1536]{1,0:T(8,128)(2,1)}) %reduce-scatter.3.cloned.1.call-update) | async-done | bytes 786448 | tf_op jit(solution)/shard_map/reduce_scatter | solution.py:302
  228.8 0.0 all-to-all-done.3
  228.8 17.8 %all_to_all.22 = bf16[4,64,1536]{2,1,0:T(8,128)(2,1)S(1)} all-to-all(bf16[4,64,1536]{2,1,0:T(8,128)(2,1)} %bitcast.22), channel_id=1, replica_groups=mesh['rep'=1,'dp'=4,'ad'=8] {'dp'}, dimensions={0} | all-to-all | bytes 1572864 | tf_op jit(solution)/shard_map/all_to_all | solution.py:303
  246.5 0.0 copy-start.1
  246.5 0.1 pad_maximum_fusion
  246.7 0.5 copy-done.1
  247.2 2.2 convolution_convert_fusion
  (1 shorter events, 0.0 us)
Async XLA Ops:
  6.5 62.7 %all-gather.5.cloned.1.call-start = ((), (), s32[]{:S(2)}) async-start(), calls=%async_computation.8 | async-start | bytes 7667712 | tf_op jit(solution)/shard_map/all_gather | solution.py:299
  8.3 2.7 %copy-start = (s32[512]{0:T(512)}, s32[512]{0:T(512)S(1)}, u32[]{:S(2)}) copy-start(s32[512]{0:T(512)S(1)} %fusion.8) | copy-start | bytes 6148
  30.0 99.5 %all-gather.3.cloned.1.call-start = ((), (), s32[]{:S(2)}) async-start(), calls=%async_computation.6 | async-start | bytes 7667712 | tf_op jit(solution)/shard_map/all_gather | solution.py:299
  45.5 144.2 %reduce-scatter.5.cloned.1.call-start = ((), (), s32[]{:S(2)}) async-start(), calls=%async_computation.9 | async-start | bytes 7077888 | tf_op jit(solution)/shard_map/reduce_scatter | solution.py:302
  129.2 99.5 %reduce-scatter.3.cloned.1.call-start = ((), (), s32[]{:S(2)}) async-start(), calls=%async_computation.7 | async-start | bytes 7077888 | tf_op jit(solution)/shard_map/reduce_scatter | solution.py:302
  189.7 39.1 %all-to-all-start.3 = ((bf16[4,64,1536]{2,1,0:T(8,128)(2,1)}), bf16[4,64,1536]{2,1,0:T(8,128)(2,1)S(1)}, u32[]{:S(2)}, u32[]{:S(2)}) async-start(bf16[4,64,1536]{2,1,0:T(8,128)(2,1)} %bitcast.21), calls=%async_computation.5 | async-start | bytes 1572864 | tf_op jit(solution)/shard_map/all_to_all | solution.py:303
  246.5 0.7 copy-start.1
Sparse Core Ops, SparseCore 0:
  30.1 39.0 all-gather.4
  70.8 40.4 all-gather.2
  129.4 38.9 reduce-scatter.4
  189.8 38.9 reduce-scatter.2

commit v3 on v2

--- a/solution.py
+++ b/solution.py
@@ -268,6 +268,124 @@
       a_up, b_up.reshape(n_groups, depth, d_ff), a_down, b_down.reshape(n_groups, depth, d_model))
 
 
+def spread_kernel(rows_ref, pool_ref, later_ref, send_sem, recv_sem, own_sem):
+    n_ad, n_dp, part, _ = pool_ref.shape
+    n_later = later_ref.shape[0]
+    half = part // 2
+    dp, ad = lax.axis_index("dp"), lax.axis_index("ad")
+    core = lax.rem(ad, 2)
+    other = ad + 1 - 2 * core
+    right = lax.rem(ad + 2, n_ad)
+    left = lax.rem(ad + n_ad - 2, n_ad)
+    far = lax.rem(ad + 4, n_ad)
+
+    barrier = pltpu.get_barrier_semaphore()
+    peers = [{"dp": lax.rem(dp + r, n_dp)} for r in range(1, n_dp)] + [{"ad": right}, {"ad": left}, {"ad": other}]
+    for peer in peers:
+        pl.semaphore_signal(barrier, inc=1, device_id=peer, device_id_type=pl.DeviceIdType.MESH)
+    pl.semaphore_wait(barrier, len(peers))
+
+    def remote(kind, r, src, dst, peer):
+        return pltpu.make_async_remote_copy(
+            src_ref=src, dst_ref=dst, send_sem=send_sem.at[kind, r], recv_sem=recv_sem.at[kind, r],
+            device_id=peer, device_id_type=pl.DeviceIdType.MESH)
+
+    def source(r):
+        return lax.rem(dp + n_dp - r, n_dp)
+
+    def across(phase, r):
+        to = lax.rem(dp + r, n_dp)
+        dst = pool_ref.at[ad, dp] if phase == 0 else later_ref.at[phase - 1, dp]
+        return remote(9 + phase, r, rows_ref.at[phase, to], dst, {"dp": to})
+
+    def whole(kind, r, block, peer):
+        src = rows_ref.at[0, dp] if r == 0 and kind in (0, 1, 2) else pool_ref.at[block, source(r)]
+        return remote(kind, r, src, pool_ref.at[block, source(r)], peer)
+
+    def halved(kind, r, block, which, peer):
+        at = pool_ref.at[block, source(r), pl.ds(which * half, half), :]
+        return remote(kind, r, at, at, peer)
+
+    def near(r):
+        return [whole(0, r, ad, {"ad": right}), whole(1, r, ad, {"ad": left}), whole(2, r, ad, {"ad": other})]
+
+    def on_right(r):
+        return [halved(3, r, left, 0, {"ad": right}), whole(4, r, left, {"ad": other})]
+
+    def on_left(r):
+        return [halved(5, r, right, 1, {"ad": left}), whole(6, r, right, {"ad": other})]
+
+    def on_far(r, which):
+        return [halved(7 + which, r, far, which, {"ad": other})]
+
+    def start(copies):
+        for copy in copies:
+            copy.start()
+
+    own = [pltpu.make_async_copy(rows_ref.at[0, dp], pool_ref.at[ad, dp], own_sem.at[0])]
+    own += [pltpu.make_async_copy(rows_ref.at[p + 1, dp], later_ref.at[p, dp], own_sem.at[p + 1]) for p in range(n_later)]
+    order = [0] + sorted(range(1, n_dp), key=lambda r: min(r, n_dp - r))
+    start(near(0))
+    for r in order[1:]:
+        across(0, r).start()
+    start(own)
+    for phase in range(1, n_later + 1):
+        for r in order[1:]:
+            across(phase, r).start()
+
+    def hand_on(r):
+        near(r)[0].wait_recv()
+        start(on_right(r))
+        near(r)[1].wait_recv()
+        start(on_left(r))
+
+    def hand_over(r):
+        on_right(r)[0].wait_recv()
+        start(on_far(r, 0))
+        on_left(r)[0].wait_recv()
+        start(on_far(r, 1))
+
+    for n in range(n_dp + 2):
+        if 0 < n < n_dp:
+            across(0, order[n]).wait_recv()
+            start(near(order[n]))
+        if 0 <= n - 1 < n_dp:
+            hand_on(order[n - 1])
+        if 0 <= n - 2 < n_dp:
+            hand_over(order[n - 2])
+    for copy in own:
+        copy.wait()
+    for r in order:
+        copies = near(r) + on_right(r) + on_left(r) + on_far(r, 0) + on_far(r, 1)
+        for copy in copies:
+            copy.wait_send()
+        for copy in (near(r)[2], on_right(r)[1], on_left(r)[1], on_far(r, 0)[0], on_far(r, 1)[0]):
+            copy.wait_recv()
+        if r:
+            across(0, r).wait_send()
+            for phase in range(1, n_later + 1):
+                across(phase, r).wait()
+
+
+def run_spread(tagged, n_ad):
+    phases, n_dp, part, width = tagged.shape
+    kinds = 9 + phases
+    hbm = pl.BlockSpec(memory_space=pl.ANY)
+    return pl.pallas_call(
+        spread_kernel,
+        out_shape=(jax.ShapeDtypeStruct((n_ad, n_dp, part, width), tagged.dtype),
+                   jax.ShapeDtypeStruct((phases - 1, n_dp, part, width), tagged.dtype)),
+        in_specs=[pl.BlockSpec(memory_space=pltpu.VMEM)],
+        out_specs=(hbm, hbm),
+        scratch_shapes=[
+            pltpu.SemaphoreType.DMA((kinds, n_dp)),
+            pltpu.SemaphoreType.DMA((kinds, n_dp)),
+            pltpu.SemaphoreType.DMA((phases,)),
+        ],
+        compiler_params=pltpu.CompilerParams(collective_id=0, has_side_effects=True),
+    )(tagged)
+
+
 def spread_order(adapter_id, parts):
     n_rows = adapter_id.shape[0]
     index = jnp.arange(n_rows)
@@ -278,7 +396,7 @@
 
 
 def solution(mesh):
-    n_dp = mesh.shape["dp"]
+    n_dp, n_ad = mesh.shape["dp"], mesh.shape["ad"]
     tok_axes = ("rep", "dp", "ad")
     row_spec = P(tok_axes, None)
     owned = P("ad", None, None)
@@ -295,8 +413,9 @@
         tagged = tagged.reshape(PHASES, n_dp, part, d_model + LANES)
         first = (lax.axis_index("ad") * n_local).astype(jnp.int32).reshape(1)
         back = []
-        spread = [lax.all_to_all(tagged[ph], "dp", 0, 0) for ph in range(PHASES)]
-        pools = [lax.all_gather(s.reshape(n_dp * part, -1), "ad", axis=0, tiled=True) for s in spread]
+        pool, later = run_spread(tagged, n_ad)
+        pools = [pool.reshape(n_ad * n_dp * part, -1)]
+        pools += [lax.all_gather(later[p].reshape(n_dp * part, -1), "ad", axis=0, tiled=True) for p in range(PHASES - 1)]
         done = [run_owner(pool, first, *weights) for pool in pools]
         for d in done:
             mine = lax.psum_scatter(d, "ad", scatter_dimension=0, tiled=True)

time: 256 us -> 239 us (0.934)
  Pallas kernels: 120 us -> 161 us
  waiting for transfers between devices: 58.4 us -> 21.6 us
  blocking collectives: 51.9 us -> 34.1 us
  starting transfers between devices: 4.93 us -> 0.53 us
    pallas_call x0 -> x1, Pallas kernels: none -> 40.9 us  [run_spread(): pl.pallas_call(spread_kernel, out_shape=(jax.ShapeDtypeStruct((n_ad, n_dp...]
    all_to_all x2 -> x0, blocking collectives: 34.2 us -> none  [local_step(): spread = [lax.all_to_all(tagged[ph], 'dp', 0, 0) for ph in range(PHASES)]]
    all_gather x2 -> x1, waiting for transfers between devices: 23.4 us -> 0.02 us  [local_step(): lax.all_gather(later[p].reshape(n_dp * part, -1), 'ad', axis=0, tiled=True)]
    all_to_all x1 -> x2, blocking collectives: 17.8 us -> 34.1 us  [local_step(): back.append(lax.all_to_all(mine.reshape(n_dp, part, d_model), 'dp', 0, 0))]
    reduce_scatter x2, waiting for transfers between devices: 34.7 us -> 21.4 us  [local_step(): mine = lax.psum_scatter(d, 'ad', scatter_dimension=0, tiled=True)]
    all_to_all x1 -> x0, starting transfers between devices: 4.33 us -> none  [local_step(): back.append(lax.all_to_all(mine.reshape(n_dp, part, d_model), 'dp', 0, 0))]
  transfers between devices with their start and end apart: 5 -> 3, of which waited for: 2 -> 1; matrix products, arithmetic and copies ran while one was open for 0% -> 0% of each run, Pallas kernels for 47% -> 50%
where the time goes in v3:
time: 239 us
  Pallas kernels  161 us (67%)
  blocking collectives  34.1 us (14%)
  waiting for transfers between devices  21.6 us (9%)
  between operations  13.2 us (6%)
  matrix products  5.93 us (2%)
    pallas_call x2, Pallas kernels, run_owner(): pl.pallas_call(functools.partial(owner_mlp, scale=LORA_ALPHA / rank, n_lo...  120 us
    pallas_call x1, Pallas kernels, run_spread(): pl.pallas_call(spread_kernel, out_shape=(jax.ShapeDtypeStruct((n_ad, n_dp...  40.9 us
    all_to_all x2, blocking collectives, local_step(): back.append(lax.all_to_all(mine.reshape(n_dp, part, d_model), 'dp', 0, 0))  34.1 us
    reduce_scatter x2, waiting for transfers between devices, local_step(): mine = lax.psum_scatter(d, 'ad', scatter_dimension=0, tiled=True)  21.4 us
  transfers between devices with their start and end apart: 3, of which 1 were waited for; matrix products, arithmetic and copies ran while one was open for 0% of the time, Pallas kernels for 50%

profile of v3, /device:TPU:98, one launch (start us, length us, event | category | flops | bytes accessed | tf_op | source)
XLA Modules:
  0.0 238.8 jit_solution(9109471648113494030)
XLA Ops:
  6.5 0.0 all-gather.2.cloned.1.call-start
  6.6 0.7 convert_element_type.14
  7.2 1.1 convert_reduce_fusion
  8.3 0.0 copy-start
  8.3 0.1 broadcast_in_dim.2
  8.5 3.7 %convolution_convert_fusion.1 = bf16[512,1664]{1,0:T(8,128)(2,1)} fusion(bf16[512,128]{1,0:T(8,128)(2,1)S(1)} %broadcast_in_dim.2, bf16[512,1536]{1,0:T(8,128)(2,1)} %param.11, s32[512]{0:T(512)S(1)} %fusion.8), kind=kOutput, calls=%fused_computation.1 | convolution fusion | flops 876937216 | bytes 3409920 | tf_op jit(solution)/shard_map/dot_general | solution.py:412
  12.2 0.0 copy-done
  12.2 40.9 %shard_map.109 = (bf16[8,4,64,1664]{3,2,1,0:T(8,128)(2,1)}, bf16[1,4,64,1664]{3,2,1,0:T(8,128)(2,1)}) custom-call(bf16[2,4,64,1664]{3,2,1,0:T(8,128)(2,1)} %bitcast.15), custom_call_target="tpu_custom_call" | custom-call | tf_op jit(solution)/shard_map/pallas_call | solution.py:374
  53.1 0.1 all-gather.2.cloned.1.call-update
  53.2 0.2 reduce-scatter.3.cloned.1.call-start
  53.5 60.0 %shard_map.110 = bf16[2048,1536]{1,0:T(8,128)(2,1)} custom-call(s32[1]{0:T(128)} %bitcast.first_ref, bf16[2048,1664]{1,0:T(8,128)(2,1)} %bitcast.24, bf16[1536,8960]{1,0:T(8,128)(2,1)} %wg_hbm.3, bf16[1536,8960]{1,0:T(8,128)(2,1)} %wu_hbm.3, bf16[8960,1536]{1,0:T(8,128)(2,1)} %wd_hbm.3, bf16[4,1536,128]{2,1,0:T(8,128)(2,1)} %ag_hbm.3, ...), custom_call_target="tpu_custom_call" | custom-call | flops 37899730944 | bytes 140000000 | tf_op jit(solution)/shard_map/pallas_call | solution.py:236
  113.5 0.1 reduce-scatter.3.cloned.1.call-update
  113.5 0.3 reduce-scatter.5.cloned.1.call-start
  113.8 0.0 all-gather.2.cloned.1.call-done.pool_hbm
  113.9 60.0 %shard_map.111 = bf16[2048,1536]{1,0:T(8,128)(2,1)} custom-call(s32[1]{0:T(128)} %bitcast.first_ref, bf16[2048,1664]{1,0:T(8,128)(2,1)} %all-gather.2.cloned.1.call-done.pool_hbm, bf16[1536,8960]{1,0:T(8,128)(2,1)} %wg_hbm.3, bf16[1536,8960]{1,0:T(8,128)(2,1)} %wu_hbm.3, bf16[8960,1536]{1,0:T(8,128)(2,1)} %wd_hbm.3, bf16[4,1536,128]{2,1,0:T(8,128)(2,1)} %ag_hbm.3, ...), custom_call_target="tpu_custom_call" | custom-call | flops 37899730944 | bytes 140000000 | tf_op jit(solution)/shard_map/pallas_call | solution.py:236
  173.9 0.1 reduce-scatter.5.cloned.1.call-update
  173.9 0.0 reduce-scatter.3.cloned.1.call-done
  174.0 16.3 %all_to_all.10 = bf16[4,64,1536]{2,1,0:T(8,128)(2,1)S(1)} all-to-all(bf16[4,64,1536]{2,1,0:T(8,128)(2,1)} %bitcast.18), channel_id=1, replica_groups=mesh['rep'=1,'dp'=4,'ad'=8] {'dp'}, dimensions={0} | all-to-all | bytes 1572864 | tf_op jit(solution)/shard_map/all_to_all | solution.py:422
  190.3 21.4 %reduce-scatter.5.cloned.1.call-done = bf16[256,1536]{1,0:T(8,128)(2,1)} async-done(((bf16[2048,1536]{1,0:T(8,128)(2,1)}), bf16[256,1536]{1,0:T(8,128)(2,1)}) %reduce-scatter.5.cloned.1.call-update) | async-done | bytes 786448 | tf_op jit(solution)/shard_map/reduce_scatter | solution.py:421
  211.7 17.7 %all_to_all.11 = bf16[4,64,1536]{2,1,0:T(8,128)(2,1)S(1)} all-to-all(bf16[4,64,1536]{2,1,0:T(8,128)(2,1)} %bitcast.19), channel_id=1, replica_groups=mesh['rep'=1,'dp'=4,'ad'=8] {'dp'}, dimensions={0} | all-to-all | bytes 1572864 | tf_op jit(solution)/shard_map/all_to_all | solution.py:422
  229.4 0.0 copy-start.1
  229.4 0.1 pad_maximum_fusion
  229.6 0.5 copy-done.1
  230.1 2.2 convolution_convert_fusion
  (1 shorter events, 0.0 us)
Async XLA Ops:
  6.5 107.3 %all-gather.2.cloned.1.call-start = ((), (), s32[]{:S(2)}) async-start(), calls=%async_computation.5 | async-start | bytes 7667712 | tf_op jit(solution)/shard_map/all_gather | solution.py:418
  8.3 3.9 %copy-start = (s32[512]{0:T(512)}, s32[512]{0:T(512)S(1)}, u32[]{:S(2)}) copy-start(s32[512]{0:T(512)S(1)} %fusion.8) | copy-start | bytes 6148
  53.2 120.7 %reduce-scatter.3.cloned.1.call-start = ((), (), s32[]{:S(2)}) async-start(), calls=%async_computation.4 | async-start | bytes 7077888 | tf_op jit(solution)/shard_map/reduce_scatter | solution.py:421
  113.5 98.1 %reduce-scatter.5.cloned.1.call-start = ((), (), s32[]{:S(2)}) async-start(), calls=%async_computation.6 | async-start | bytes 7077888 | tf_op jit(solution)/shard_map/reduce_scatter | solution.py:421
  229.4 0.7 copy-start.1
Sparse Core Ops, SparseCore 0:
  53.3 39.0 all-gather.1
  113.7 37.6 reduce-scatter.2
  174.0 37.5 reduce-scatter.4

commit v4 on v3

--- a/solution.py
+++ b/solution.py
@@ -64,16 +64,19 @@
     before = jnp.zeros((8, BLOCK), f32)
     for b in range(n_blocks):
         load_block(b).wait()
-    for copy in fixed:
-        copy.start()
-    for copy in stream(0, 0):
-        copy.start()
+        if b == n_blocks // 2:
+            for copy in fixed + stream(0, 0):
+                copy.start()
+    ids = lax.dot_general(lane, pool[:, d_model:], (((1,), (1,)), ((), ())), preferred_element_type=f32)
+    mine = []
     for b in range(n_blocks):
-        ids = lax.dot_general(lane, pool[block_rows(b), d_model:], (((1,), (1,)), ((), ())), preferred_element_type=f32)
-        local = ids - first - lowest
-        mine = (local >= 0.0) & (local < per_group) & (group < n_groups)
-        upto = jnp.dot(jnp.where(mine, 1.0, 0.0).astype(bf16), upper, preferred_element_type=f32)
-        place = jnp.where(mine, upto + (before - 1.0), -1e6)
+        local = ids[:, b * BLOCK:(b + 1) * BLOCK] - first - lowest
+        mine.append((local >= 0.0) & (local < per_group) & (group < n_groups))
+    ones = jnp.concatenate([jnp.where(m, 1.0, 0.0) for m in mine], axis=0).astype(bf16)
+    counts = jnp.dot(ones, upper, preferred_element_type=f32)
+    for b in range(n_blocks):
+        upto = counts[8 * b:8 * (b + 1), :]
+        place = jnp.where(mine[b], upto + (before - 1.0), -1e6)
         for g in range(n_groups):
             relative[g, b:b + 1, :] = place[g:g + 1, :]
         before = before + jnp.broadcast_to(upto[:, BLOCK - 1:], (8, BLOCK))
@@ -386,6 +389,38 @@
     )(tagged)
 
 
+def return_kernel(rows_ref, out_ref, send_sem, recv_sem, own_sem):
+    n_dp = rows_ref.shape[0]
+    dp = lax.axis_index("dp")
+    barrier = pltpu.get_barrier_semaphore()
+    for r in range(1, n_dp):
+        pl.semaphore_signal(barrier, inc=1, device_id={"dp": lax.rem(dp + r, n_dp)},
+                            device_id_type=pl.DeviceIdType.MESH)
+    pl.semaphore_wait(barrier, n_dp - 1)
+    copies = [pltpu.make_async_copy(rows_ref.at[dp], out_ref.at[dp], own_sem)]
+    for r in sorted(range(1, n_dp), key=lambda r: -min(r, n_dp - r)):
+        to = lax.rem(dp + r, n_dp)
+        copies.append(pltpu.make_async_remote_copy(
+            src_ref=rows_ref.at[to], dst_ref=out_ref.at[dp], send_sem=send_sem.at[r], recv_sem=recv_sem.at[r],
+            device_id={"dp": to}, device_id_type=pl.DeviceIdType.MESH))
+    for copy in copies[1:] + copies[:1]:
+        copy.start()
+    for copy in copies:
+        copy.wait()
+
+
+def run_return(rows):
+    n_dp = rows.shape[0]
+    return pl.pallas_call(
+        return_kernel,
+        out_shape=jax.ShapeDtypeStruct(rows.shape, rows.dtype),
+        in_specs=[pl.BlockSpec(memory_space=pltpu.VMEM)],
+        out_specs=pl.BlockSpec(memory_space=pl.ANY),
+        scratch_shapes=[pltpu.SemaphoreType.DMA((n_dp,)), pltpu.SemaphoreType.DMA((n_dp,)), pltpu.SemaphoreType.DMA],
+        compiler_params=pltpu.CompilerParams(collective_id=1, has_side_effects=True),
+    )(rows)
+
+
 def spread_order(adapter_id, parts):
     n_rows = adapter_id.shape[0]
     index = jnp.arange(n_rows)
@@ -417,9 +452,9 @@
         pools = [pool.reshape(n_ad * n_dp * part, -1)]
         pools += [lax.all_gather(later[p].reshape(n_dp * part, -1), "ad", axis=0, tiled=True) for p in range(PHASES - 1)]
         done = [run_owner(pool, first, *weights) for pool in pools]
-        for d in done:
-            mine = lax.psum_scatter(d, "ad", scatter_dimension=0, tiled=True)
-            back.append(lax.all_to_all(mine.reshape(n_dp, part, d_model), "dp", 0, 0))
+        for ph, d in enumerate(done):
+            mine = lax.psum_scatter(d, "ad", scatter_dimension=0, tiled=True).reshape(n_dp, part, d_model)
+            back.append(run_return(mine) if ph == PHASES - 1 else lax.all_to_all(mine, "dp", 0, 0))
         back = jnp.stack(back).reshape(n_rows, d_model)
         return jnp.dot(move.T, back, preferred_element_type=jnp.float32).astype(x_rows.dtype)
 

time: 239 us -> 237 us (level)
  blocking collectives: 34.1 us -> 0 us
  Pallas kernels: 161 us -> 175 us
  waiting for transfers between devices: 21.6 us -> 34.3 us
  starting transfers between devices: 0.53 us -> 4.13 us
    all_to_all x2 -> x0, blocking collectives: 34.1 us -> none  [local_step(): back.append(lax.all_to_all(mine.reshape(n_dp, part, d_model), 'dp', 0, 0))]
    pallas_call x0 -> x1, Pallas kernels: none -> 15.2 us  [run_return(): pl.pallas_call(return_kernel, out_shape=jax.ShapeDtypeStruct(rows.shape,...]
    reduce_scatter x2, waiting for transfers between devices: 21.4 us -> 34.1 us  [local_step(): lax.psum_scatter(d, 'ad', scatter_dimension=0, tiled=True)]
    all_to_all x0 -> x1, starting transfers between devices: none -> 3.6 us  [local_step(): lax.all_to_all(mine, 'dp', 0, 0)]
  transfers between devices with their start and end apart: 3 -> 4, of which waited for: 1 -> 1; matrix products, arithmetic and copies ran while one was open for 0% -> 0% of each run, Pallas kernels for 50% -> 57%
where the time goes in v4:
time: 237 us; the launch traced here: 235 us
  Pallas kernels  175 us (74%)
  waiting for transfers between devices  34.3 us (14%)
  between operations  13.2 us (6%)
  matrix products  5.94 us (3%)
  starting transfers between devices  4.13 us (2%)
  other arithmetic  3.05 us (1%)
    pallas_call x2, Pallas kernels, run_owner(): pl.pallas_call(functools.partial(owner_mlp, scale=LORA_ALPHA / rank, n_lo...  118 us
    pallas_call x1, Pallas kernels, run_spread(): pl.pallas_call(spread_kernel, out_shape=(jax.ShapeDtypeStruct((n_ad, n_dp...  40.9 us
    reduce_scatter x2, waiting for transfers between devices, local_step(): lax.psum_scatter(d, 'ad', scatter_dimension=0, tiled=True)  34.1 us
    pallas_call x1, Pallas kernels, run_return(): pl.pallas_call(return_kernel, out_shape=jax.ShapeDtypeStruct(rows.shape,...  15.2 us
  transfers between devices with their start and end apart: 4, of which 1 were waited for; matrix products, arithmetic and copies ran while one was open for 0% of the time, Pallas kernels for 57%

profile of v4, /device:TPU:98, one launch (start us, length us, event | category | flops | bytes accessed | tf_op | source)
XLA Modules:
  0.0 235.4 jit_solution(1259449020242822062)
XLA Ops:
  6.5 0.0 all-gather.2.cloned.1.call-start
  6.6 0.7 convert_element_type.14
  7.2 1.1 convert_reduce_fusion
  8.3 0.0 copy-start
  8.3 0.1 broadcast_in_dim.2
  8.5 3.7 %convolution_convert_fusion.1 = bf16[512,1664]{1,0:T(8,128)(2,1)} fusion(bf16[512,128]{1,0:T(8,128)(2,1)S(1)} %broadcast_in_dim.2, bf16[512,1536]{1,0:T(8,128)(2,1)} %param.11, s32[512]{0:T(512)S(1)} %fusion.8), kind=kOutput, calls=%fused_computation.1 | convolution fusion | flops 876937216 | bytes 3409920 | tf_op jit(solution)/shard_map/dot_general | solution.py:447
  12.2 0.0 copy-done
  12.2 40.9 %shard_map.109 = (bf16[8,4,64,1664]{3,2,1,0:T(8,128)(2,1)}, bf16[1,4,64,1664]{3,2,1,0:T(8,128)(2,1)}) custom-call(bf16[2,4,64,1664]{3,2,1,0:T(8,128)(2,1)} %bitcast.15), custom_call_target="tpu_custom_call" | custom-call | tf_op jit(solution)/shard_map/pallas_call | solution.py:377
  53.1 0.1 all-gather.2.cloned.1.call-update
  53.2 0.2 reduce-scatter.3.cloned.1.call-start
  53.5 59.2 %shard_map.110 = bf16[2048,1536]{1,0:T(8,128)(2,1)} custom-call(s32[1]{0:T(128)} %bitcast.first_ref, bf16[2048,1664]{1,0:T(8,128)(2,1)} %bitcast.24, bf16[1536,8960]{1,0:T(8,128)(2,1)} %wg_hbm.3, bf16[1536,8960]{1,0:T(8,128)(2,1)} %wu_hbm.3, bf16[8960,1536]{1,0:T(8,128)(2,1)} %wd_hbm.3, bf16[4,1536,128]{2,1,0:T(8,128)(2,1)} %ag_hbm.3, ...), custom_call_target="tpu_custom_call" | custom-call | flops 37899730944 | bytes 140000000 | tf_op jit(solution)/shard_map/pallas_call | solution.py:239
  112.7 0.1 reduce-scatter.3.cloned.1.call-update
  112.8 0.3 reduce-scatter.5.cloned.1.call-start
  113.1 0.0 all-gather.2.cloned.1.call-done.pool_hbm
  113.1 59.3 %shard_map.111 = bf16[2048,1536]{1,0:T(8,128)(2,1)} custom-call(s32[1]{0:T(128)} %bitcast.first_ref, bf16[2048,1664]{1,0:T(8,128)(2,1)} %all-gather.2.cloned.1.call-done.pool_hbm, bf16[1536,8960]{1,0:T(8,128)(2,1)} %wg_hbm.3, bf16[1536,8960]{1,0:T(8,128)(2,1)} %wu_hbm.3, bf16[8960,1536]{1,0:T(8,128)(2,1)} %wd_hbm.3, bf16[4,1536,128]{2,1,0:T(8,128)(2,1)} %ag_hbm.3, ...), custom_call_target="tpu_custom_call" | custom-call | flops 37899730944 | bytes 140000000 | tf_op jit(solution)/shard_map/pallas_call | solution.py:239
  172.3 0.1 reduce-scatter.5.cloned.1.call-update
  172.4 0.0 reduce-scatter.3.cloned.1.call-done
  172.4 3.6 %all-to-all-start = ((bf16[4,64,1536]{2,1,0:T(8,128)(2,1)}), bf16[4,64,1536]{2,1,0:T(8,128)(2,1)S(1)}, u32[]{:S(2)}, u32[]{:S(2)}) async-start(bf16[4,64,1536]{2,1,0:T(8,128)(2,1)} %bitcast.18), calls=%async_computation.1 | async-start | bytes 1572864 | tf_op jit(solution)/shard_map/all_to_all | solution.py:457
  176.0 34.1 %reduce-scatter.5.cloned.1.call-done = bf16[256,1536]{1,0:T(8,128)(2,1)} async-done(((bf16[2048,1536]{1,0:T(8,128)(2,1)}), bf16[256,1536]{1,0:T(8,128)(2,1)}) %reduce-scatter.5.cloned.1.call-update) | async-done | bytes 786448 | tf_op jit(solution)/shard_map/reduce_scatter | solution.py:456
  210.1 15.2 %shard_map.112 = bf16[4,64,1536]{2,1,0:T(8,128)(2,1)} custom-call(bf16[4,64,1536]{2,1,0:T(8,128)(2,1)} %bitcast.19), custom_call_target="tpu_custom_call" | custom-call | tf_op jit(solution)/shard_map/pallas_call | solution.py:414
  225.3 0.0 copy-start.1
  225.3 0.0 all-to-all-done
  225.4 1.3 pad_maximum_fusion
  226.6 0.0 copy-done.1
  226.7 2.2 convolution_convert_fusion
  (1 shorter events, 0.0 us)
Async XLA Ops:
  6.5 106.5 %all-gather.2.cloned.1.call-start = ((), (), s32[]{:S(2)}) async-start(), calls=%async_computation.4 | async-start | bytes 7667712 | tf_op jit(solution)/shard_map/all_gather | solution.py:453
  8.3 3.9 %copy-start = (s32[512]{0:T(512)}, s32[512]{0:T(512)S(1)}, u32[]{:S(2)}) copy-start(s32[512]{0:T(512)S(1)} %fusion.8) | copy-start | bytes 6148
  53.2 119.2 %reduce-scatter.3.cloned.1.call-start = ((), (), s32[]{:S(2)}) async-start(), calls=%async_computation.3 | async-start | bytes 7077888 | tf_op jit(solution)/shard_map/reduce_scatter | solution.py:456
  112.8 97.4 %reduce-scatter.5.cloned.1.call-start = ((), (), s32[]{:S(2)}) async-start(), calls=%async_computation.5 | async-start | bytes 7077888 | tf_op jit(solution)/shard_map/reduce_scatter | solution.py:456
  172.4 52.9 %all-to-all-start = ((bf16[4,64,1536]{2,1,0:T(8,128)(2,1)}), bf16[4,64,1536]{2,1,0:T(8,128)(2,1)S(1)}, u32[]{:S(2)}, u32[]{:S(2)}) async-start(bf16[4,64,1536]{2,1,0:T(8,128)(2,1)} %bitcast.18), calls=%async_computation.1 | async-start | bytes 1572864 | tf_op jit(solution)/shard_map/all_to_all | solution.py:457
  225.3 1.3 copy-start.1
Sparse Core Ops, SparseCore 0:
  53.3 39.0 all-gather.1
  112.9 37.6 reduce-scatter.2
  172.5 37.5 reduce-scatter.4
